TPU v7x, 32 devices: a whole 2x2x4 slice. The times are simulated.
32 devices in a mesh: gz: 8 (over y, x, core), gy: 4 (over z).
Axes of the slice: x: 2, y: 2, z: 4, core: 2. Of those that a mesh axis runs over, the one named last changes fastest.
Arguments:
- features: bfloat16 [32, 32, 32, 256], P(None, 'gz', 'gy'), may hold values from -6 to 6
- scale_first: float32 [32], replicated, may hold values from 0.5 to 2
- shift_first: float32 [32], replicated, may hold values from -3 to 3
- conv_first: bfloat16 [3, 3, 32, 32], replicated, may hold values from -0.375 to 0.375
- bias_first: float32 [32], replicated, may hold values from -3 to 3
- scale_second: float32 [32], replicated, may hold values from 0.5 to 2
- shift_second: float32 [32], replicated, may hold values from -3 to 3
- conv_second: bfloat16 [3, 3, 32, 32], replicated, may hold values from -0.375 to 0.375
- bias_second: float32 [32], replicated, may hold values from -3 to 3
- flow_weight: bfloat16 [2, 32], replicated, may hold values from -1 to 1
Outputs:
- smoothed: float32 [3, 32, 32, 256], P(None, 'gz', 'gy')
All inputs are finite; a program needn't handle non-finite values.
Results may differ from a plain program's by a relative error of at most 0.0015.
Values may be sent and summed in bfloat16 or wider, within the bound.
No kernel may reach another device: no remote copies, remote signals or barrier semaphores. Data moves between devices by JAX's collectives and lax.ppermute only.
A program may use at most 64 MiB of HBM per device.

v0:
```python
import jax
import jax.numpy as jnp
from jax import lax
from jax.sharding import PartitionSpec as P


def extended(value, sides, width):
    for axis, dim in sides:
        devices, length = (lax.axis_size(axis), value.shape[dim])
        up = [(i, (i + 1) % devices) for i in range(devices - 1)]
        down = [(j, i) for i, j in up]
        last = lax.slice_in_dim(value, length - width, length, axis=dim)
        first = lax.slice_in_dim(value, 0, width, axis=dim)
        before = lax.ppermute(last, axis, up)
        after = lax.ppermute(first, axis, down)
        value = jnp.concatenate([before, value, after], axis=dim)
    return value


def shift_cols(source, delta):
    if delta == 0:
        return source
    zeros = jnp.zeros(source.shape[:-1] + (1,), source.dtype)
    if delta == 1:
        return jnp.concatenate([source[..., 1:], zeros], -1)
    return jnp.concatenate([zeros, source[..., :-1]], -1)


def plane_conv(source, weight, plane_axes, count_z, count_y, start_z, start_y):
    summed = None
    for row_tap in range(3):
        for col_tap in range(3):
            offset = {1: 0, 2: 0, 3: 0}
            offset[plane_axes[0]] = row_tap - 1
            offset[plane_axes[1]] = col_tap - 1
            low_z = start_z + offset[1]
            low_y = start_y + offset[2]
            window = lax.slice(
                source,
                (0, low_z, low_y, 0),
                (source.shape[0], low_z + count_z, low_y + count_y, source.shape[3]),
            )
            window = shift_cols(window, offset[3])
            term = jnp.einsum(
                "oc,czyx->ozyx",
                weight[row_tap, col_tap],
                window,
                preferred_element_type=jnp.float32,
            )
            summed = term if summed is None else summed + term
    return summed


def column(vector):
    return vector[:, None, None, None]


def inside_mask(low_z, count_z, low_y, count_y, total_z, total_y):
    place_z = low_z + jnp.arange(count_z, dtype=jnp.int32)
    place_y = low_y + jnp.arange(count_y, dtype=jnp.int32)
    inside_z = (place_z >= 0) & (place_z < total_z)
    inside_y = (place_y >= 0) & (place_y < total_y)
    return inside_z[None, :, None, None] & inside_y[None, None, :, None]


def shards(
    features,
    scale_first,
    shift_first,
    conv_first,
    bias_first,
    scale_second,
    shift_second,
    conv_second,
    bias_second,
    flow_weight,
):
    depth, rows = (features.shape[1], features.shape[2])
    first_z = lax.axis_index("gz") * depth
    first_y = lax.axis_index("gy") * rows
    total_z = depth * lax.axis_size("gz")
    total_y = rows * lax.axis_size("gy")
    flows = []
    unit = jax.nn.relu(
        features.astype(jnp.float32) * column(scale_first) + column(shift_first)
    ).astype(jnp.bfloat16)
    padded = extended(unit, (("gz", 1), ("gy", 2)), 2)
    for plane_axes in ((2, 3), (1, 3), (1, 2)):
        grow_z = 1 if 1 in plane_axes else 0
        grow_y = 1 if 2 in plane_axes else 0
        hidden = plane_conv(
            padded,
            conv_first,
            plane_axes,
            depth + 2 * grow_z,
            rows + 2 * grow_y,
            2 - grow_z,
            2 - grow_y,
        ) + column(bias_first)
        active = jax.nn.relu(hidden * column(scale_second) + column(shift_second))
        active = jnp.where(
            inside_mask(
                first_z - grow_z,
                depth + 2 * grow_z,
                first_y - grow_y,
                rows + 2 * grow_y,
                total_z,
                total_y,
            ),
            active,
            0.0,
        ).astype(jnp.bfloat16)
        output = plane_conv(active, conv_second, plane_axes, depth, rows, grow_z, grow_y)
        block = (output + column(bias_second) + features.astype(jnp.float32)).astype(jnp.bfloat16)
        flows.append(
            jnp.einsum("kc,czyx->kzyx", flow_weight, block, preferred_element_type=jnp.float32)
        )
    flow_xy, flow_xz, flow_yz = flows
    mean_flow = jnp.stack(
        [
            0.5 * (flow_xz[0] + flow_yz[0]),
            0.5 * (flow_xy[0] + flow_yz[1]),
            0.5 * (flow_xy[1] + flow_xz[1]),
        ]
    )
    ext = extended(mean_flow, (("gz", 1), ("gy", 2)), 1)
    ext = 0.25 * ext[:, :-2] + 0.5 * ext[:, 1:-1] + 0.25 * ext[:, 2:]
    ext = 0.25 * ext[:, :, :-2] + 0.5 * ext[:, :, 1:-1] + 0.25 * ext[:, :, 2:]
    return 0.25 * shift_cols(ext, -1) + 0.5 * ext + 0.25 * shift_cols(ext, 1)


def solution(mesh):
    return jax.shard_map(
        shards,
        mesh=mesh,
        in_specs=(P(None, "gz", "gy", None), P(), P(), P(), P(), P(), P(), P(), P(), P()),
        out_specs=P(None, "gz", "gy", None),
        check_vma=False,
    )
```

profile of v0, /device:TPU:19, one launch (start us, length us, event | category | flops | bytes accessed | tf_op | source)
XLA Modules:
  0.0 70.7 jit_solution(7325486932479537065)
XLA Ops:
  0.0 1.4 %fusion.28 = bf16[32,4,8,256]{3,0,2,1:T(8,128)(2,1)S(1)} fusion(f32[32]{0:T(128)} %param.12, f32[32]{0:T(128)} %param.11, bf16[32,4,8,256]{3,2,1,0:T(8,128)(2,1)} %param.10), kind=kLoop, calls=%fused_computation.71 | loop fusion | flops 1310720 | bytes 1048832 | tf_op jit(solution)/shard_map/convert_element_type | solution.py:86
  1.5 3.7 %collective-permute-start = (bf16[32,2,8,256]{3,0,2,1:T(8,128)(2,1)S(1)}, bf16[32,2,8,256]{3,0,2,1:T(8,128)(2,1)S(1)}, u32[]{:S(2)}, u32[]{:S(2)}) collective-permute-start(bf16[32,2,8,256]{3,0,2,1:T(8,128)(2,1)S(1)} %get-tuple-element.35), channel_id=1, source_target_pairs={{0,4},{4,8},{8,12},{12,16},{16,20},{20,24},{24,28},{1,5},{5,9},{9,... | collective-permute-start | bytes 786440 | tf_op jit(solution)/shard_map/ppermute | solution.py:14
  5.2 1.9 %collective-permute-start.1 = (bf16[32,2,8,256]{3,0,2,1:T(8,128)(2,1)S(1)}, bf16[32,2,8,256]{3,0,2,1:T(8,128)(2,1)S(1)}, u32[]{:S(2)}, u32[]{:S(2)}) collective-permute-start(bf16[32,2,8,256]{3,0,2,1:T(8,128)(2,1)S(1)} %get-tuple-element.36), channel_id=1, source_target_pairs={{4,0},{8,4},{12,8},{16,12},{20,16},{24,20},{28,24},{5,1},{9,5},{13... | collective-permute-start | bytes 786440 | tf_op jit(solution)/shard_map/ppermute | solution.py:15
  7.2 0.7 broadcast_and_fusion.2
  7.8 0.6 broadcast_and_fusion
  8.5 5.2 %collective-permute-done.1 = bf16[32,2,8,256]{3,0,2,1:T(8,128)(2,1)S(1)} collective-permute-done((bf16[32,2,8,256]{3,0,2,1:T(8,128)(2,1)S(1)}, bf16[32,2,8,256]{3,0,2,1:T(8,128)(2,1)S(1)}, u32[]{:S(2)}, u32[]{:S(2)}) %collective-permute-start.1) | collective-permute-done | bytes 262176 | tf_op jit(solution)/shard_map/ppermute | solution.py:15
  13.9 0.8 %fusion.285 = (bf16[32,8,2,256]{3,0,2,1:T(8,128)(2,1)}, bf16[32,8,2,256]{3,0,2,1:T(8,128)(2,1)}) fusion(bf16[32,8,8,256]{3,0,2,1:T(8,128)(2,1)S(1)} %pad_maximum_fusion.4), kind=kLoop, calls=%fused_computation.340 | loop fusion | bytes 1048576 | tf_op jit(solution)/shard_map/slice | solution.py:12
  15.2 3.2 %collective-permute-start.2 = (bf16[32,8,2,256]{3,0,2,1:T(8,128)(2,1)}, bf16[32,8,2,256]{3,0,2,1:T(8,128)(2,1)S(1)}, u32[]{:S(2)}, u32[]{:S(2)}) collective-permute-start(bf16[32,8,2,256]{3,0,2,1:T(8,128)(2,1)} %get-tuple-element.13), channel_id=1, source_target_pairs={{0,1},{1,2},{2,3},{4,5},{5,6},{6,7},{8,9},{9,10},{10,11},{12,13},{... | collective-permute-start | bytes 786440 | tf_op jit(solution)/shard_map/ppermute | solution.py:14
  18.4 2.1 %collective-permute-start.3 = (bf16[32,8,2,256]{3,0,2,1:T(8,128)(2,1)}, bf16[32,8,2,256]{3,0,2,1:T(8,128)(2,1)}, u32[]{:S(2)}, u32[]{:S(2)}) collective-permute-start(bf16[32,8,2,256]{3,0,2,1:T(8,128)(2,1)} %get-tuple-element.14), channel_id=1, source_target_pairs={{1,0},{2,1},{3,2},{5,4},{6,5},{7,6},{9,8},{10,9},{11,10},{13,12},{... | collective-permute-start | bytes 786440 | tf_op jit(solution)/shard_map/ppermute | solution.py:15
  20.8 0.8 %fusion.54 = (bf16[32,6,8,255]{3,0,2,1:T(8,128)(2,1)S(1)}, bf16[32,6,8,255]{3,0,2,1:T(8,128)(2,1)S(1)}, bf16[32,6,8,255]{3,0,2,1:T(8,128)(2,1)S(1)}, bf16[32,6,8,255]{3,0,2,1:T(8,128)(2,1)S(1)}) fusion(bf16[32,4,8,256]{3,0,2,1:T(8,128)(2,1)S(1)} %fusion.28, bf16[32,2,8,256]{3,0,2,1:T(8,128)(2,1)S(1)} %collective-permute-done, ...), kind=kLoop, calls=%fused_computation.98 | loop fusion | flops 1566720 | bytes 4182016 | tf_op jit(solution)/shard_map/concatenate | solution.py:16
  22.4 0.4 fusion.75
  24.7 0.9 %fusion.64 = bf16[32,6,8,256]{3,0,2,1:T(8,128)(2,1)S(1)} fusion(f32[32]{0:T(128)S(1)} %copy-done.5, f32[32]{0:T(128)S(1)} %copy-done.6, f32[32]{0:T(128)S(1)} %copy-done.8, bf16[32,6,8,255]{3,0,2,1:T(8,128)(2,1)S(1)} %get-tuple-element.33, f32[6,8,256,32]{2,3,1,0:T(8,128)S(1)} %fusion.56, f32[6,8,256,32]{2,3,1,0:T(8,128)S(1)} %fusion.67, ...), kind=kOutput, calls=%fused_computation.106 | convolution fusion | flops 30670848 | bytes 14166528 | tf_op jit(solution)/shard_map/oc,czyx->ozyx/dot_general | solution.py:44
  25.6 0.7 fusion.287
  29.0 0.7 %copy-done.1 = bf16[32,4,8,256]{3,2,1,0:T(8,128)(2,1)S(1)} copy-done((bf16[32,4,8,256]{3,2,1,0:T(8,128)(2,1)S(1)}, bf16[32,4,8,256]{3,2,1,0:T(8,128)(2,1)}, u32[]{:S(2)}) %copy-start.1) | copy-done | bytes 524312
  29.8 1.3 %fusion.23 = f32[2,4,8,256]{3,0,2,1:T(2,128)S(1)} fusion(f32[4,8,256,32]{2,3,1,0:T(8,128)S(1)} %convolution_add_fusion.21, f32[32]{0:T(128)} %param.18, bf16[32,4,8,255]{3,0,2,1:T(8,128)(2,1)S(1)} %get-tuple-element.17, bf16[32,4,8,256]{3,2,1,0:T(8,128)(2,1)S(1)} %copy-done.1, bf16[3,3,32,32]{3,2,1,0:T(8,128)(2,1)} %param.17, bf16[2,32]{1,0:T(2,128)(2,1)S(1)} %copy-done), kind=kOutput, calls=%fused_computation.66 | convolution fusion | flops 19136512 | bytes 2169472 | tf_op jit(solution)/shard_map/kc,czyx->kzyx/dot_general | solution.py:116
  31.1 1.2 %pad_maximum_fusion = bf16[32,8,12,256]{3,0,2,1:T(8,128)(2,1)S(1)} fusion(bf16[32,8,2,256]{3,0,2,1:T(8,128)(2,1)} %collective-permute-done.3, bf16[32,2,8,256]{3,0,2,1:T(8,128)(2,1)S(1)} %collective-permute-done.1, bf16[32,4,8,256]{3,0,2,1:T(8,128)(2,1)S(1)} %fusion.28, bf16[32,2,8,256]{3,0,2,1:T(8,128)(2,1)S(1)} %collective-permute-done, ...), kind=kLoop, calls=%fused_computation.5 | loop fusion | flops 3145728 | bytes 3145728 | tf_op jit(solution)/shard_map/concatenate | solution.py:16
  33.0 1.5 %maximum_maximum_fusion = (bf16[32,8,10,256]{3,0,2,1:T(8,128)(2,1)S(1)}, bf16[32,8,10,256]{3,0,2,1:T(8,128)(2,1)S(1)}) fusion(bf16[32,2,8,256]{3,0,2,1:T(8,128)(2,1)S(1)} %collective-permute-done.1, bf16[32,4,8,256]{3,0,2,1:T(8,128)(2,1)S(1)} %fusion.28, bf16[32,2,8,256]{3,0,2,1:T(8,128)(2,1)S(1)} %collective-permute-done, ...), kind=kLoop, calls=%fused_computation.51 | loop fusion | flops 3932160 | bytes 4194304 | tf_op jit(solution)/shard_map/concatenate | solution.py:16
  35.2 0.7 fusion.283
  40.4 0.6 fusion.8
  41.1 0.5 fusion.19
  41.6 0.7 fusion.288
  45.4 1.2 %fusion.33 = bf16[32,6,10,256]{3,0,2,1:T(8,128)(2,1)S(1)} fusion(bf16[32,8,10,256]{3,0,2,1:T(8,128)(2,1)S(1)} %get-tuple-element.12, f32[6,10,256,32]{2,3,1,0:T(8,128)S(1)} %fusion.36, f32[6,10,256,32]{2,3,1,0:T(8,128)S(1)} %fusion.38, f32[6,10,256,32]{2,3,1,0:T(8,128)S(1)} %fusion.40, f32[6,10,256,32]{2,3,1,0:T(8,128)S(1)} %fusion.42, ...), kind=kOutput, calls=%fused_computation.75 | convolution fusion | flops 38338560 | bytes 17705472 | tf_op jit(solution)/shard_map/oc,czyx->ozyx/dot_general | solution.py:44
  48.5 1.3 %convolution_add_fusion.13 = f32[4,8,256,32]{2,3,1,0:T(8,128)} fusion(f32[4,8,256,32]{2,3,1,0:T(8,128)S(1)} %convolution_add_fusion.14, bf16[32,6,10,256]{3,0,2,1:T(8,128)(2,1)S(1)} %fusion.33, bf16[3,3,32,32]{3,2,1,0:T(8,128)(2,1)S(1)} %copy-done.4), kind=kOutput, calls=%fused_computation.33 | convolution fusion | flops 17039360 | bytes 2629632 | tf_op jit(solution)/shard_map/oc,czyx->ozyx/dot_general | solution.py:44
  49.8 1.9 %fusion.24 = f32[2,4,8,256]{3,0,2,1:T(2,128)S(1)} fusion(f32[4,8,256,32]{2,3,1,0:T(8,128)} %convolution_add_fusion.13, bf16[32,6,10,256]{3,0,2,1:T(8,128)(2,1)S(1)} %fusion.33, f32[32]{0:T(128)S(1)} %copy-done.10, bf16[32,4,8,256]{3,2,1,0:T(8,128)(2,1)S(1)} %copy-done.1, bf16[3,3,32,32]{3,2,1,0:T(8,128)(2,1)S(1)} %copy-done.4, bf16[2,32]{1,0:T(2,128)(2,1)S(1)} %copy-done), kind=kOutput, calls=%fused_computation.67 | convolution fusion | flops 19136512 | bytes 2171904 | tf_op jit(solution)/shard_map/kc,czyx->kzyx/dot_general | solution.py:116
  51.7 0.7 fusion.25
  52.5 2.3 %collective-permute-start.4 = (f32[3,1,8,256]{3,0,2,1:T(4,128)S(1)}, f32[3,1,8,256]{3,0,2,1:T(4,128)S(1)}, u32[]{:S(2)}, u32[]{:S(2)}) collective-permute-start(f32[3,1,8,256]{3,0,2,1:T(4,128)S(1)} %get-tuple-element.41), channel_id=1, source_target_pairs={{0,4},{4,8},{8,12},{12,16},{16,20},{20,24},{24,28},{1,5},{5,9},{9,... | collective-permute-start | bytes 73736 | tf_op jit(solution)/shard_map/ppermute | solution.py:14
  54.8 2.0 %collective-permute-start.5 = (f32[3,1,8,256]{3,0,2,1:T(4,128)S(1)}, f32[3,1,8,256]{3,0,2,1:T(4,128)S(1)}, u32[]{:S(2)}, u32[]{:S(2)}) collective-permute-start(f32[3,1,8,256]{3,0,2,1:T(4,128)S(1)} %get-tuple-element.42), channel_id=1, source_target_pairs={{4,0},{8,4},{12,8},{16,12},{20,16},{24,20},{28,24},{5,1},{9,5},{13... | collective-permute-start | bytes 73736 | tf_op jit(solution)/shard_map/ppermute | solution.py:15
  56.9 4.1 %collective-permute-done.5 = f32[3,1,8,256]{3,0,2,1:T(4,128)S(1)} collective-permute-done((f32[3,1,8,256]{3,0,2,1:T(4,128)S(1)}, f32[3,1,8,256]{3,0,2,1:T(4,128)S(1)}, u32[]{:S(2)}, u32[]{:S(2)}) %collective-permute-start.5) | collective-permute-done | bytes 24608 | tf_op jit(solution)/shard_map/ppermute | solution.py:15
  61.0 3.9 %collective-permute-start.6 = (f32[3,6,1,256]{3,0,2,1:T(4,128)S(1)}, f32[3,6,1,256]{3,0,2,1:T(4,128)S(1)}, u32[]{:S(2)}, u32[]{:S(2)}) collective-permute-start(f32[3,6,1,256]{3,0,2,1:T(4,128)S(1)} %get-tuple-element.37), channel_id=1, source_target_pairs={{0,1},{1,2},{2,3},{4,5},{5,6},{6,7},{8,9},{9,10},{10,11},{12,13},{... | collective-permute-start | bytes 55304 | tf_op jit(solution)/shard_map/ppermute | solution.py:14
  64.9 1.9 %collective-permute-start.7 = (f32[3,6,1,256]{3,0,2,1:T(4,128)S(1)}, f32[3,6,1,256]{3,0,2,1:T(4,128)S(1)}, u32[]{:S(2)}, u32[]{:S(2)}) collective-permute-start(f32[3,6,1,256]{3,0,2,1:T(4,128)S(1)} %get-tuple-element.38), channel_id=1, source_target_pairs={{1,0},{2,1},{3,2},{5,4},{6,5},{7,6},{9,8},{10,9},{11,10},{13,12},{... | collective-permute-start | bytes 55304 | tf_op jit(solution)/shard_map/ppermute | solution.py:15
  66.9 2.6 %collective-permute-done.7 = f32[3,6,1,256]{3,0,2,1:T(4,128)S(1)} collective-permute-done((f32[3,6,1,256]{3,0,2,1:T(4,128)S(1)}, f32[3,6,1,256]{3,0,2,1:T(4,128)S(1)}, u32[]{:S(2)}, u32[]{:S(2)}) %collective-permute-start.7) | collective-permute-done | bytes 18464 | tf_op jit(solution)/shard_map/ppermute | solution.py:15
  70.0 0.7 copy.12
  (92 shorter events, 17.7 us)
Async XLA Ops:
  0.0 29.0 %copy-start = (bf16[2,32]{1,0:T(2,128)(2,1)S(1)}, bf16[2,32]{1,0:T(2,128)(2,1)}, u32[]{:S(2)}) copy-start(bf16[2,32]{1,0:T(2,128)(2,1)} %param.19) | copy-start | bytes 388
  1.5 7.0 %collective-permute-start = (bf16[32,2,8,256]{3,0,2,1:T(8,128)(2,1)S(1)}, bf16[32,2,8,256]{3,0,2,1:T(8,128)(2,1)S(1)}, u32[]{:S(2)}, u32[]{:S(2)}) collective-permute-start(bf16[32,2,8,256]{3,0,2,1:T(8,128)(2,1)S(1)} %get-tuple-element.35), channel_id=1, source_target_pairs={{0,4},{4,8},{8,12},{12,16},{16,20},{20,24},{24,28},{1,5},{5,9},{9,... | collective-permute-start | bytes 786440 | tf_op jit(solution)/shard_map/ppermute | solution.py:14
  5.2 8.6 %collective-permute-start.1 = (bf16[32,2,8,256]{3,0,2,1:T(8,128)(2,1)S(1)}, bf16[32,2,8,256]{3,0,2,1:T(8,128)(2,1)S(1)}, u32[]{:S(2)}, u32[]{:S(2)}) collective-permute-start(bf16[32,2,8,256]{3,0,2,1:T(8,128)(2,1)S(1)} %get-tuple-element.36), channel_id=1, source_target_pairs={{4,0},{8,4},{12,8},{16,12},{20,16},{24,20},{28,24},{5,1},{9,5},{13... | collective-permute-start | bytes 786440 | tf_op jit(solution)/shard_map/ppermute | solution.py:15
  14.7 5.7 %copy-start.2 = (bf16[3,3,32,32]{3,2,1,0:T(8,128)(2,1)S(1)}, bf16[3,3,32,32]{3,2,1,0:T(8,128)(2,1)}, u32[]{:S(2)}) copy-start(bf16[3,3,32,32]{3,2,1,0:T(8,128)(2,1)} %param.13) | copy-start | bytes 55300
  15.2 16.0 %collective-permute-start.2 = (bf16[32,8,2,256]{3,0,2,1:T(8,128)(2,1)}, bf16[32,8,2,256]{3,0,2,1:T(8,128)(2,1)S(1)}, u32[]{:S(2)}, u32[]{:S(2)}) collective-permute-start(bf16[32,8,2,256]{3,0,2,1:T(8,128)(2,1)} %get-tuple-element.13), channel_id=1, source_target_pairs={{0,1},{1,2},{2,3},{4,5},{5,6},{6,7},{8,9},{9,10},{10,11},{12,13},{... | collective-permute-start | bytes 786440 | tf_op jit(solution)/shard_map/ppermute | solution.py:14
  18.4 12.8 %collective-permute-start.3 = (bf16[32,8,2,256]{3,0,2,1:T(8,128)(2,1)}, bf16[32,8,2,256]{3,0,2,1:T(8,128)(2,1)}, u32[]{:S(2)}, u32[]{:S(2)}) collective-permute-start(bf16[32,8,2,256]{3,0,2,1:T(8,128)(2,1)} %get-tuple-element.14), channel_id=1, source_target_pairs={{1,0},{2,1},{3,2},{5,4},{6,5},{7,6},{9,8},{10,9},{11,10},{13,12},{... | collective-permute-start | bytes 786440 | tf_op jit(solution)/shard_map/ppermute | solution.py:15
  24.0 0.7 copy-start.5
  24.0 0.7 copy-start.6
  24.0 0.7 copy-start.8
  25.6 0.9 %copy-start.3 = (bf16[3,3,32,32]{3,2,1,0:T(8,128)(2,1)S(1)}, bf16[3,3,32,32]{3,2,1,0:T(8,128)(2,1)}, u32[]{:S(2)}) copy-start(bf16[3,3,32,32]{3,2,1,0:T(8,128)(2,1)} %param.17) | copy-start | bytes 55300
  28.7 1.0 %copy-start.1 = (bf16[32,4,8,256]{3,2,1,0:T(8,128)(2,1)S(1)}, bf16[32,4,8,256]{3,2,1,0:T(8,128)(2,1)}, u32[]{:S(2)}) copy-start(bf16[32,4,8,256]{3,2,1,0:T(8,128)(2,1)} %param.10) | copy-start | bytes 1572868
  40.4 0.7 copy-start.7
  40.4 0.7 copy-start.9
  40.4 0.7 copy-start.12
  41.6 0.9 %copy-start.4 = (bf16[3,3,32,32]{3,2,1,0:T(8,128)(2,1)S(1)}, bf16[3,3,32,32]{3,2,1,0:T(8,128)(2,1)}, u32[]{:S(2)}) copy-start(bf16[3,3,32,32]{3,2,1,0:T(8,128)(2,1)} %param.17) | copy-start | bytes 55300
  44.7 0.7 copy-start.11
  48.5 1.3 %copy-start.10 = (f32[32]{0:T(128)S(1)}, f32[32]{0:T(128)}, u32[]{:S(2)}) copy-start(f32[32]{0:T(128)} %param.18) | copy-start | bytes 388
  52.5 4.3 %collective-permute-start.4 = (f32[3,1,8,256]{3,0,2,1:T(4,128)S(1)}, f32[3,1,8,256]{3,0,2,1:T(4,128)S(1)}, u32[]{:S(2)}, u32[]{:S(2)}) collective-permute-start(f32[3,1,8,256]{3,0,2,1:T(4,128)S(1)} %get-tuple-element.41), channel_id=1, source_target_pairs={{0,4},{4,8},{8,12},{12,16},{16,20},{20,24},{24,28},{1,5},{5,9},{9,... | collective-permute-start | bytes 73736 | tf_op jit(solution)/shard_map/ppermute | solution.py:14
  54.8 6.1 %collective-permute-start.5 = (f32[3,1,8,256]{3,0,2,1:T(4,128)S(1)}, f32[3,1,8,256]{3,0,2,1:T(4,128)S(1)}, u32[]{:S(2)}, u32[]{:S(2)}) collective-permute-start(f32[3,1,8,256]{3,0,2,1:T(4,128)S(1)} %get-tuple-element.42), channel_id=1, source_target_pairs={{4,0},{8,4},{12,8},{16,12},{20,16},{24,20},{28,24},{5,1},{9,5},{13... | collective-permute-start | bytes 73736 | tf_op jit(solution)/shard_map/ppermute | solution.py:15
  61.0 5.9 %collective-permute-start.6 = (f32[3,6,1,256]{3,0,2,1:T(4,128)S(1)}, f32[3,6,1,256]{3,0,2,1:T(4,128)S(1)}, u32[]{:S(2)}, u32[]{:S(2)}) collective-permute-start(f32[3,6,1,256]{3,0,2,1:T(4,128)S(1)} %get-tuple-element.37), channel_id=1, source_target_pairs={{0,1},{1,2},{2,3},{4,5},{5,6},{6,7},{8,9},{9,10},{10,11},{12,13},{... | collective-permute-start | bytes 55304 | tf_op jit(solution)/shard_map/ppermute | solution.py:14
  64.9 4.6 %collective-permute-start.7 = (f32[3,6,1,256]{3,0,2,1:T(4,128)S(1)}, f32[3,6,1,256]{3,0,2,1:T(4,128)S(1)}, u32[]{:S(2)}, u32[]{:S(2)}) collective-permute-start(f32[3,6,1,256]{3,0,2,1:T(4,128)S(1)} %get-tuple-element.38), channel_id=1, source_target_pairs={{1,0},{2,1},{3,2},{5,4},{6,5},{7,6},{9,8},{10,9},{11,10},{13,12},{... | collective-permute-start | bytes 55304 | tf_op jit(solution)/shard_map/ppermute | solution.py:15
where the time goes:
time: 71.3 us; the launch traced here: 70.7 us
  matrix products  23.7 us (33%)
  starting transfers between devices  21.1 us (30%)
  waiting for transfers between devices  11.9 us (17%)
  other arithmetic  7.03 us (10%)
  local copies, waits for them, and re-layouts  6.32 us (9%)
    dot_general x51, matrix products, plane_conv(): jnp.einsum('oc,czyx->ozyx', weight[row_tap, col_tap], window, preferred_e...  19.8 us
    ppermute x4, starting transfers between devices, extended(): before = lax.ppermute(last, axis, up)  13.1 us
    ppermute x4, waiting for transfers between devices, extended(): after = lax.ppermute(first, axis, down)  11.9 us
    ppermute x4, starting transfers between devices, extended(): after = lax.ppermute(first, axis, down)  7.97 us
    dot_general x3, matrix products, shards(): jnp.einsum('kc,czyx->kzyx', flow_weight, block, preferred_element_type=jn...  3.88 us
    concatenate x5, other arithmetic, extended(): value = jnp.concatenate([before, value, after], axis=dim)  3.74 us
    slice x3, local copies, waits for them, and re-layouts, shift_cols(): return jnp.concatenate([source[..., 1:], zeros], -1)  2.04 us
    unnamed x26, local copies, waits for them, and re-layouts  1.86 us
  transfers between devices with their start and end apart: 8, of which 3 were waited for; matrix products, arithmetic and copies ran while one was open for 15% of the time, Pallas kernels for 0%

commit v1 on v0

v1 whole, which is shorter than its diff:
```python
import functools

import jax
import jax.numpy as jnp
from jax import lax
from jax.experimental import pallas as pl
from jax.experimental.pallas import tpu as pltpu
from jax.sharding import PartitionSpec as P


HALO = 3
SPAN = 6
WIDE = SPAN + 2
F32, BF16 = jnp.float32, jnp.bfloat16
VMEM = pl.BlockSpec(memory_space=pltpu.VMEM)
HBM = pl.BlockSpec(memory_space=pltpu.HBM)


def iota(shape, dim):
    return lax.broadcasted_iota(jnp.int32, shape, dim)


def matmul(a, b):
    return jnp.dot(a, b, preferred_element_type=F32)


def swap(value, axis, first):
    pairs = []
    for i in range(first, lax.axis_size(axis) - 1, 2):
        pairs += [(i, i + 1), (i + 1, i)]
    return lax.ppermute(value, axis, pairs)


def call(kernel, outs, args, flops, mib, scratch=(), space=VMEM):
    nbytes = sum(a.size * a.dtype.itemsize for a in (*outs, *args))
    return pl.pallas_call(
        kernel,
        out_shape=outs,
        in_specs=[space] * len(args),
        out_specs=[VMEM] * len(outs),
        scratch_shapes=list(scratch),
        cost_estimate=pl.CostEstimate(flops=flops, bytes_accessed=nbytes, transcendentals=0),
        compiler_params=pltpu.CompilerParams(vmem_limit_bytes=mib * 2**20),
    )(*args)


def odd(axis):
    return lax.rem(lax.axis_index(axis), 2)


def pack_kernel(feat_ref, own_ref, far_ref, even_ref, odd_ref):
    channels, depth, rows, cols = feat_ref.shape
    size = channels * rows
    row, col = iota((size, size), 0), iota((size, size), 1)
    order = ((row // channels == col % rows) & (row % channels == col // rows)).astype(F32).astype(BF16)
    part_z, part_y = odd("gz"), odd("gy")
    for z in range(depth):
        value = feat_ref[:, z].astype(F32).reshape(size, cols).astype(BF16)
        value = matmul(order, value).astype(BF16).reshape(rows, channels, cols)
        own_ref[part_z * z + (1 - part_z) * (depth - 1 - z)] = value
    first_even, first_odd = (1 - part_y) * (rows - HALO), part_y * (rows - HALO)
    for layer in range(HALO):
        far_ref[layer] = own_ref[depth - 1 - layer]
    for z in range(depth):
        for row in range(HALO):
            even_ref[z, row] = own_ref[z, first_even + row]
            odd_ref[z, row] = own_ref[z, first_odd + row]


def rim_kernel(own_ref, even_ref, odd_ref, near_ref, corner_ref):
    depth, rows = own_ref.shape[:2]
    for layer in range(HALO):
        near_ref[layer, :rows] = own_ref[layer]
        near_ref[layer, rows : rows + HALO] = even_ref[layer]
        near_ref[layer, rows + HALO :] = odd_ref[layer]
        corner_ref[layer, :HALO] = even_ref[depth - 1 - layer]
        corner_ref[layer, HALO:] = odd_ref[depth - 1 - layer]


def weights_kernel(
    scale1_hbm, shift1_hbm, conv1_hbm, bias1_hbm, scale2_hbm, shift2_hbm, conv2_hbm, bias2_hbm, flow_hbm,
    wxy_ref, wyz_ref, wza_ref, wzb_ref, vxy_ref, vyz_ref, vza_ref, vzb_ref, vf_ref,
    s1_ref, t1_ref, s2_ref, t2_ref, const_ref,
    scale1, shift1, conv1, bias1, scale2, shift2, conv2, bias2, flow, taps, folds, sem,
):
    copies = [
        pltpu.make_async_copy(source, target, sem.at[n])
        for n, (source, target) in enumerate(
            (
                (scale1_hbm, scale1), (shift1_hbm, shift1), (conv1_hbm, conv1), (bias1_hbm, bias1),
                (scale2_hbm, scale2), (shift2_hbm, shift2), (conv2_hbm, conv2), (bias2_hbm, bias2), (flow_hbm, flow),
            )
        )
    ]
    for copy in copies:
        copy.start()
    for copy in copies:
        copy.wait()
    c = conv1.shape[-1]
    part_z = odd("gz")

    def along_z(i):
        return part_z * i + (1 - part_z) * (2 - i)

    def spread(vector, rows, cols):
        pick = iota((rows, c), 0) % c == iota((rows, c), 1)
        column = jnp.sum(jnp.where(pick, vector, 0.0), axis=1, keepdims=True)
        return jnp.broadcast_to(column, (rows, cols))

    s1_ref[...] = spread(scale1[...], *s1_ref.shape)
    t1_ref[...] = spread(shift1[...], *t1_ref.shape)
    s2_ref[...] = spread(scale2[...], *s2_ref.shape)
    t2_ref[...] = spread(bias1[...] * scale2[...] + shift2[...], *t2_ref.shape)
    const = jnp.sum(flow[...].astype(F32) * bias2[...], axis=1, keepdims=True)
    half = const_ref.shape[0] // 2
    for k in range(2):
        const_ref[k * half : (k + 1) * half] = jnp.broadcast_to(const[k : k + 1], (half, const_ref.shape[1]))

    def tile_of(cols):
        return (iota((c, cols), 0) == iota((c, cols), 1) % c).astype(F32).astype(BF16)

    tile = tile_of(taps.shape[-1])
    short = tile_of(folds.shape[-1])
    for i in range(3):
        for j in range(3):
            taps[i, j] = matmul(conv1[i, j], tile)
            both = matmul(flow[...], conv2[i, j])
            high = both.astype(BF16)
            low = (both - high.astype(F32)).astype(BF16)
            folds[i, j, 0] = matmul(high, short)
            folds[i, j, 1] = matmul(low, short)

    def banded(ref, pick):
        rows, cols = ref.shape
        group = cols // 3
        lane = iota((c, cols), 1)
        slot = lane % group // c
        for a in range(rows // c):
            value = jnp.zeros((c, cols), F32)
            for g in range(3):
                for i in range(3):
                    value = jnp.where((slot == a + i) & (lane // group == g), pick(g, i)[:, :cols], value)
            ref[a * c : (a + 1) * c] = value.astype(BF16)

    banded(wxy_ref, lambda g, i: taps[i, g])
    banded(wyz_ref, lambda g, i: taps[along_z(g), i])
    banded(wza_ref, lambda g, i: taps[along_z(i), g])
    banded(wzb_ref, lambda g, i: taps[along_z(i), g])

    def banded_flow(ref, pick, skip):
        cols = ref.shape[1]
        height = ref.shape[0] // 12
        band = iota((height, cols), 1) // c + skip - iota((height, cols), 0)
        for part in range(2):
            for g in range(3):
                for k in range(2):
                    block = jnp.zeros((height, cols), F32)
                    for i in range(3):
                        row, col = pick(g, i)
                        block = jnp.where(band == i, folds[row, col, part, k : k + 1, :cols], block)
                    at = ((part * 3 + g) * 2 + k) * height
                    ref[at : at + height] = block.astype(BF16)

    banded_flow(vxy_ref, lambda g, i: (i, g), 0)
    banded_flow(vyz_ref, lambda g, i: (along_z(g), i), 0)
    banded_flow(vza_ref, lambda g, i: (along_z(i), g), 0)
    banded_flow(vzb_ref, lambda g, i: (along_z(i), g), vza_ref.shape[1] // c)
    cols = vf_ref.shape[1]
    plain = matmul(flow[...], short)
    for k in range(2):
        band = iota((half, cols), 1) // c - iota((half, cols), 0)
        vf_ref[k * half : (k + 1) * half] = jnp.where(band == 0, plain[k : k + 1, :cols], 0.0).astype(BF16)


def shift_right(value):
    return jnp.where(iota(value.shape, 1) == 0, 0.0, pltpu.roll(value, 1, 1))


def shift_left(value):
    last = value.shape[1] - 1
    return jnp.where(iota(value.shape, 1) == last, 0.0, pltpu.roll(value, last, 1))


def valid_sides():
    part_z = odd("gz")
    low = (lax.axis_index("gz") > 0).astype(F32)
    high = (lax.axis_index("gz") < lax.axis_size("gz") - 1).astype(F32)
    near = jnp.where(part_z == 1, low, high)
    far = jnp.where(part_z == 1, high, low)
    low_y = (lax.axis_index("gy") > 0).astype(F32)
    high_y = (lax.axis_index("gy") < lax.axis_size("gy") - 1).astype(F32)
    return near, far, low_y, high_y


def y_halos(rows, low_y, high_y):
    part_y = odd("gy")
    valid_even = jnp.where(part_y == 1, low_y, high_y)
    valid_odd = jnp.where(part_y == 1, high_y, low_y)
    return ((1 - part_y) * (rows + HALO), valid_even), (part_y * (rows + HALO), valid_odd)


def normalized(value, s1, t1, valid):
    count, c, cols = value.shape
    size = count * c
    value = jnp.maximum(value.reshape(size, cols).astype(F32) * s1[:size] + t1[:size], 0.0)
    if valid is not None:
        value = value * valid
    return [v.astype(BF16).reshape(count, c, cols) for v in (shift_right(value), value, shift_left(value))]


def set_masks(sm, tm, s2, t2, low_y, high_y):
    size, cols = s2.shape
    c = size // SPAN
    row = iota((size, cols), 0)
    for n, keep in enumerate((row >= 2 * c, row < size - 2 * c)):
        keep = jnp.where(keep, 1.0, high_y if n else low_y)
        sm[n] = s2[...] * keep
        tm[n] = t2[...] * keep


def activate(hidden, scale, shift, c, valid=None):
    value = jnp.maximum(hidden * scale + shift, 0.0)
    if valid is not None:
        value = value * valid
    return value.astype(BF16).reshape(-1, c, value.shape[1])


def stack(pieces):
    return jnp.concatenate([p.reshape(-1, p.shape[-1]) for p in pieces], axis=0)


def two_parts(value):
    half = value.shape[0] // 2
    return value[:half] + value[half:]


def along_x(value):
    value = two_parts(value)
    step = value.shape[0] // 3
    return shift_right(value[:step]) + value[step : 2 * step] + shift_left(value[2 * step :])


def planes(
    unit, xy_layers, out_layers, out_xz, data_xz, edge_xz,
    wxy, wyz, wz, vxy, vyz, vz, s2, t2, sm, tm, act_xy, act_yz, act_xz, fxz, outer,
):
    c, cols = act_xy.shape[-2:]
    wide = act_xy.shape[1]
    flow_xy, flow_yz = {}, {}
    for n, z in enumerate(xy_layers):
        for w in range(wide // SPAN):
            data = stack([unit(j, z, slice(w * SPAN, w * SPAN + WIDE)) for j in range(3)])
            act_xy[n, w * SPAN : (w + 1) * SPAN] = activate(matmul(wxy[...], data), sm[w], tm[w], c)
    for n, z in enumerate(out_layers):
        for w in range(wide // SPAN):
            data = stack([unit(1, z + i - 1, slice(w * SPAN, w * SPAN + WIDE)) for i in range(3)])
            act_yz[n, w * SPAN : (w + 1) * SPAN] = activate(matmul(wyz[...], data), sm[w], tm[w], c, outer(z))
    count = len(out_xz)
    row = iota((count * c, cols), 0)
    keep = jnp.where((row >= edge_xz[0] * c) & (row < edge_xz[1] * c), edge_xz[2], 1.0)
    scale, shift = s2[: count * c] * keep, t2[: count * c] * keep
    for y in range(act_xz.shape[0]):
        data = stack([unit(j, z, y + 2) for j in range(3) for z in data_xz])
        act_xz[y] = activate(matmul(wz[...], data), scale, shift, c)
    for y in range(act_xz.shape[0]):
        flow = along_x(matmul(vz[...], act_xz[y].reshape(-1, cols)))
        half = flow.shape[0] // 2
        for k in range(2):
            fxz[k, :, y, :] = flow[k * half : (k + 1) * half]
    for n, z in enumerate(xy_layers):
        flow_xy[z] = along_x(matmul(vxy[...], act_xy[n].reshape(-1, cols)))
    for n, z in enumerate(out_layers):
        value = two_parts(matmul(vyz[...], act_yz[n].reshape(-1, cols)))
        step = value.shape[0] // 3
        flow_yz[z] = [value[i * step : (i + 1) * step] for i in range(3)]
    return flow_xy, flow_yz


def gather_mean(add, layer, fxz, flow_xy, flow_yz, base, height):
    at = layer - 2
    parts = [0.5 * fxz[0, at], None, 0.5 * fxz[1, at]]

    def plus(k, value):
        parts[k] = value if parts[k] is None else parts[k] + value

    for i in range(3):
        if layer + i - 1 in flow_yz:
            piece = 0.5 * flow_yz[layer + i - 1][i]
            plus(0, piece[:height])
            plus(1, piece[height:])
    if layer in flow_xy:
        piece = 0.5 * flow_xy[layer]
        plus(1, piece[:height])
        plus(2, piece[height:])
    if base is not None:
        plus(0, base[:height])
        plus(1, 0.5 * (base[:height] + base[height:]))
        plus(2, base[height:])
    for k in range(3):
        if parts[k] is not None:
            add(k, at, parts[k])


def near_kernel(
    own, near, yeven, yodd, wxy, wyz, wz, vxy, vyz, vz, vf, s1, t1, s2, t2, const,
    mean, tail, unit, feat, act_xy, act_yz, act_xz, sm, tm, fxz,
):
    depth, rows, _, cols = own.shape
    valid_near, _, low_y, high_y = valid_sides()
    (at_even, valid_even), (at_odd, valid_odd) = y_halos(rows, low_y, high_y)
    first = HALO + depth - 2

    def place(value, z, y, valid):
        count = value.shape[0]
        if z >= HALO - 1:
            feat[z - HALO + 1, pl.ds(y, count)] = value
        for j, moved in enumerate(normalized(value, s1, t1, valid)):
            if z < first:
                unit[j, z, pl.ds(y, count)] = moved
            else:
                tail[j, z - first, pl.ds(y, count)] = moved

    for z in range(depth):
        place(own[z], HALO + z, HALO, None)
        place(yeven[z], HALO + z, at_even, valid_even)
        place(yodd[z], HALO + z, at_odd, valid_odd)
    for z in range(HALO):
        place(near[z, :rows], HALO - 1 - z, HALO, valid_near)
        place(near[z, rows : rows + HALO], HALO - 1 - z, at_even, valid_near * valid_even)
        place(near[z, rows + HALO :], HALO - 1 - z, at_odd, valid_near * valid_odd)
    set_masks(sm, tm, s2, t2, low_y, high_y)

    def read(j, z, y):
        return unit[j, z, y] if z < first else tail[j, z - first, y]

    outs = list(range(1, depth + 2))
    flow_xy, flow_yz = planes(
        read, list(range(2, depth + 3)), outs, outs, list(range(depth + 3)), (0, 2, valid_near),
        wxy, wyz, wz, vxy, vyz, vz, s2, t2, sm, tm, act_xy, act_yz, act_xz, fxz,
        lambda z: valid_near if z < HALO else None,
    )
    height = mean.shape[2]

    def store(k, at, value):
        mean[k, at] = value

    for layer in range(2, depth + 3):
        base = matmul(vf[...], feat[layer - 2, 2 : rows + 4].reshape(-1, cols)) + const[...]
        gather_mean(store, layer, fxz, flow_xy, flow_yz, base, height)


def far_kernel(
    far, corner, tail, mean, wxy, wyz, wz, vxy, vyz, vz, vf, s1, t1, s2, t2, const,
    out, unit, act_xy, act_yz, act_xz, sm, tm, fxz, feat, total,
):
    _, depth, rows, cols = out.shape
    valid_near, valid_far, low_y, high_y = valid_sides()
    (at_even, valid_even), (at_odd, valid_odd) = y_halos(rows, low_y, high_y)
    start = HALO + depth
    first = start - 2

    def place(value, z, y, valid):
        count = value.shape[0]
        if z == 0:
            feat[pl.ds(y, count)] = value
        for j, moved in enumerate(normalized(value, s1, t1, valid)):
            unit[j, z, pl.ds(y, count)] = moved

    for z in range(HALO):
        place(far[z], z, HALO, valid_far)
        place(corner[z, :HALO], z, at_even, valid_far * valid_even)
        place(corner[z, HALO:], z, at_odd, valid_far * valid_odd)
    set_masks(sm, tm, s2, t2, low_y, high_y)

    def read(j, z, y):
        return unit[j, z - start, y] if z >= start else tail[j, z - first, y]

    outs = list(range(start - 1, start + 2))
    flow_xy, flow_yz = planes(
        read, [start], outs, outs, list(range(first, start + HALO)), (1, 3, valid_far),
        wxy, wyz, wz, vxy, vyz, vz, s2, t2, sm, tm, act_xy, act_yz, act_xz, fxz,
        lambda z: valid_far if z >= start else None,
    )
    height = mean.shape[2]
    spot = iota((height, cols), 0)
    inside_y = jnp.where(spot == 0, low_y, jnp.where(spot == rows + 1, high_y, jnp.where(spot < rows + 1, 1.0, 0.0)))

    def store(k, at, value):
        if at < depth + 1:
            value = value + mean[k, at]
        total[k, at] = value * (inside_y * valid_far if at == depth + 1 else inside_y)

    for k in range(3):
        for at in range(depth - 1):
            total[k, at] = mean[k, at] * (inside_y * valid_near if at == 0 else inside_y)
    for layer in range(first, start + 1):
        base = None
        if layer == start:
            base = matmul(vf[...], feat[2 : rows + 4].reshape(-1, cols)) + const[...]
        gather_mean(store, layer, fxz, flow_xy, flow_yz, base, height)
    part_z = odd("gz")
    for k in range(3):
        for z in range(depth):
            value = 0.25 * (total[k, z] + total[k, z + 2]) + 0.5 * total[k, z + 1]
            value = 0.25 * (value[:rows] + value[2 : rows + 2]) + 0.5 * value[1 : rows + 1]
            value = 0.25 * (shift_right(value) + shift_left(value)) + 0.5 * value
            out[k, part_z * z + (1 - part_z) * (depth - 1 - z)] = value


def shards(
    features, scale_first, shift_first, conv_first, bias_first,
    scale_second, shift_second, conv_second, bias_second, flow_weight,
):
    c, depth, rows, cols = features.shape
    shape = jax.ShapeDtypeStruct
    cells = functools.partial(shape, dtype=BF16)
    side = cells((depth, HALO, c, cols))
    own, send_far, send_even, send_odd = call(
        pack_kernel,
        [cells((depth, rows, c, cols)), cells((HALO, rows, c, cols)), side, side],
        [features], 2 * features.size * c * rows, 6,
    )
    far = swap(send_far, "gz", 1)
    yeven = swap(send_even, "gy", 0)
    yodd = swap(send_odd, "gy", 1)

    broad = rows + 2 * HALO
    high = -(-(rows + 2) // 8) * 8
    deep = -(-(depth + 2) // 8) * 8
    params = [
        scale_first[None], shift_first[None], conv_first, bias_first[None],
        scale_second[None], shift_second[None], conv_second, bias_second[None], flow_weight,
    ]
    params = [pltpu.with_memory_space_constraint(p, pltpu.HBM) for p in params]
    wxy, wyz, wza, wzb, vxy, vyz, vza, vzb, *rest = call(
        weights_kernel,
        [
            cells((SPAN * c, 3 * WIDE * c)),
            cells((SPAN * c, 3 * WIDE * c)),
            cells(((depth + 1) * c, 3 * (depth + 3) * c)),
            cells((HALO * c, 3 * (HALO + 2) * c)),
            cells((12 * high, (rows + 4) * c)),
            cells((12 * high, (rows + 4) * c)),
            cells((12 * deep, (depth + 1) * c)),
            cells((12 * deep, HALO * c)),
            cells((2 * high, (rows + 2) * c)),
            shape((rows * c, cols), F32),
            shape((rows * c, cols), F32),
            shape((SPAN * c, cols), F32),
            shape((SPAN * c, cols), F32),
            shape((2 * high, cols), F32),
        ],
        params,
        2 * 10**9, 10,
        [
            *(pltpu.VMEM(p.shape, p.dtype) for p in params),
            pltpu.VMEM((3, 3, c, 3 * WIDE * c), F32),
            pltpu.VMEM((3, 3, 2, 2, (rows + 4) * c), F32),
            pltpu.SemaphoreType.DMA((len(params),)),
        ],
        HBM,
    )
    send_near, send_corner = call(
        rim_kernel,
        [cells((HALO, broad, c, cols)), cells((HALO, 2 * HALO, c, cols))],
        [own, yeven, yodd], 10**6, 5,
    )
    corner = swap(send_corner, "gz", 1)
    near = swap(send_near, "gz", 0)

    def scratch(layers_xy, layers_out):
        return [
            pltpu.VMEM((layers_xy, rows + 4, c, cols), BF16),
            pltpu.VMEM((layers_out, rows + 4, c, cols), BF16),
            pltpu.VMEM((rows + 2, layers_out, c, cols), BF16),
            pltpu.VMEM((2, SPAN * c, cols), F32),
            pltpu.VMEM((2, SPAN * c, cols), F32),
            pltpu.VMEM((2, deep, high, cols), F32),
        ]

    mean, tail = call(
        near_kernel,
        [shape((3, depth + 1, high, cols), F32), cells((3, 2, broad, c, cols))],
        [own, near, yeven, yodd, wxy, wyz, wza, vxy, vyz, vza, *rest],
        6 * 10**9, 24,
        [
            pltpu.VMEM((3, depth + 1, broad, c, cols), BF16),
            pltpu.VMEM((depth + 1, broad, c, cols), BF16),
            *scratch(depth + 1, depth + 1),
        ],
    )
    (out,) = call(
        far_kernel,
        [shape((3, depth, rows, cols), F32)],
        [far, corner, tail, mean, wxy, wyz, wzb, vxy, vyz, vzb, *rest],
        2 * 10**9, 16,
        [
            pltpu.VMEM((3, HALO, broad, c, cols), BF16),
            *scratch(1, HALO),
            pltpu.VMEM((broad, c, cols), BF16),
            pltpu.VMEM((3, depth + 2, high, cols), F32),
        ],
    )
    return out


def solution(mesh):
    return jax.shard_map(
        shards,
        mesh=mesh,
        in_specs=(P(None, "gz", "gy", None), P(), P(), P(), P(), P(), P(), P(), P(), P()),
        out_specs=P(None, "gz", "gy", None),
        check_vma=False,
    )
```

time: 71.3 us -> 35.2 us (0.49)
  matrix products: 23.7 us -> 0 us
  Pallas kernels: 0 us -> 11 us
  starting transfers between devices: 21.1 us -> 11.6 us
  other arithmetic: 7.03 us -> 0 us
  local copies, waits for them, and re-layouts: 6.32 us -> 1.04 us
    dot_general x54 -> x0, matrix products: 23.7 us -> none  [the longest x51 19.8 us: plane_conv(): jnp.einsum('oc,czyx->ozyx', weight[row_tap, col_tap], window, preferred_e...]
    pallas_call x0 -> x5, Pallas kernels: none -> 11 us  [call(): pl.pallas_call(kernel, out_shape=outs, in_specs=[space] * len(args), out_...]
    ppermute x8 -> x5, starting transfers between devices: 21.1 us -> 11.6 us  [swap(): return lax.ppermute(value, axis, pairs)]
    slice x8 -> x0, local copies, waits for them, and re-layouts: 3.8 us -> none  [the longest x3 2.04 us: shift_cols(): return jnp.concatenate([source[..., 1:], zeros], -1)]
    concatenate x5 -> x0, other arithmetic: 3.74 us -> none  [extended(): value = jnp.concatenate([before, value, after], axis=dim)]
    convert_element_type x1 -> x0, other arithmetic: 1.44 us -> none  [shards(): unit = jax.nn.relu(features.astype(jnp.float32) * column(scale_first) + c...]
    and x7 -> x0, other arithmetic: 1.39 us -> none  [the longest x3 1.36 us: inside_mask(): return inside_z[None, :, None, None] & inside_y[None, None, :, None]]
    unnamed x26 -> x2, local copies, waits for them, and re-layouts: 1.86 us -> 1.04 us
  transfers between devices with their start and end apart: 8 -> 5, of which waited for: 3 -> 3; matrix products, arithmetic and copies ran while one was open for 15% -> 0% of each run, Pallas kernels for 0% -> 22%
where the time goes in v1:
time: 35.2 us; the launch traced here: 34.9 us
  starting transfers between devices  11.6 us (33%)
  waiting for transfers between devices  11.2 us (32%)
  Pallas kernels  11 us (31%)
  local copies, waits for them, and re-layouts  1.04 us (3%)
    ppermute x5, starting transfers between devices, swap(): return lax.ppermute(value, axis, pairs)  11.6 us
    ppermute x5, waiting for transfers between devices, swap(): return lax.ppermute(value, axis, pairs)  11.2 us
    pallas_call x5, Pallas kernels, call(): pl.pallas_call(kernel, out_shape=outs, in_specs=[space] * len(args), out_...  11 us
    unnamed x2, local copies, waits for them, and re-layouts  1.04 us
  transfers between devices with their start and end apart: 5, of which 3 were waited for; matrix products, arithmetic and copies ran while one was open for 0% of the time, Pallas kernels for 22%

profile of v1, /device:TPU:19, one launch (start us, length us, event | category | flops | bytes accessed | tf_op | source)
XLA Modules:
  0.0 34.9 jit_solution(994895774583997217)
XLA Ops:
  0.0 0.0 copy-start
  0.0 1.0 %copy-done = bf16[32,4,8,256]{3,2,1,0:T(8,128)(2,1)S(1)} copy-done((bf16[32,4,8,256]{3,2,1,0:T(8,128)(2,1)S(1)}, bf16[32,4,8,256]{3,2,1,0:T(8,128)(2,1)}, u32[]{:S(2)}) %copy-start) | copy-done | bytes 524312
  1.0 0.4 %shard_map.100 = (bf16[4,8,32,256]{3,2,1,0:T(8,128)(2,1)S(1)}, bf16[3,8,32,256]{3,2,1,0:T(8,128)(2,1)S(1)}, bf16[4,3,32,256]{3,2,1,0:T(8,128)(2,1)S(1)}, bf16[4,3,32,256]{3,2,1,0:T(8,128)(2,1)S(1)}) custom-call(bf16[32,4,8,256]{3,2,1,0:T(8,128)(2,1)S(1)} %copy-done), custom_call_target="tpu_custom_call" | custom-call | flops 134217728 | bytes 1835008 | tf_op jit(solution)/shard_map/pallas_call | solution.py:36
  1.5 1.4 %collective-permute-start.1 = (bf16[4,3,32,256]{3,2,1,0:T(8,128)(2,1)S(1)}, bf16[4,3,32,256]{3,2,1,0:T(8,128)(2,1)S(1)}, u32[]{:S(2)}, u32[]{:S(2)}) collective-permute-start(bf16[4,3,32,256]{3,2,1,0:T(8,128)(2,1)S(1)} %get-tuple-element.29), channel_id=1, source_target_pairs={{0,1},{1,0},{2,3},{3,2},{4,5},{5,4},{6,7},{7,6},{8,9},{9,8},{10,11... | collective-permute-start | bytes 589832 | tf_op jit(solution)/shard_map/ppermute | solution.py:31
  2.8 1.9 %collective-permute-start.2 = (bf16[4,3,32,256]{3,2,1,0:T(8,128)(2,1)S(1)}, bf16[4,3,32,256]{3,2,1,0:T(8,128)(2,1)S(1)}, u32[]{:S(2)}, u32[]{:S(2)}) collective-permute-start(bf16[4,3,32,256]{3,2,1,0:T(8,128)(2,1)S(1)} %get-tuple-element.30), channel_id=1, source_target_pairs={{1,2},{2,1},{5,6},{6,5},{9,10},{10,9},{13,14},{14,13},{17,18},{18,... | collective-permute-start | bytes 589832 | tf_op jit(solution)/shard_map/ppermute | solution.py:31
  4.7 2.6 %collective-permute-done.1.even_ref.yeven = bf16[4,3,32,256]{3,2,1,0:T(8,128)(2,1)S(1)} collective-permute-done((bf16[4,3,32,256]{3,2,1,0:T(8,128)(2,1)S(1)}, bf16[4,3,32,256]{3,2,1,0:T(8,128)(2,1)S(1)}, u32[]{:S(2)}, u32[]{:S(2)}) %collective-permute-start.1) | collective-permute-done | bytes 196640 | tf_op jit(solution)/shard_map/ppermute | solution.py:31
  7.3 2.9 %collective-permute-done.2.odd_ref.yodd = bf16[4,3,32,256]{3,2,1,0:T(8,128)(2,1)S(1)} collective-permute-done((bf16[4,3,32,256]{3,2,1,0:T(8,128)(2,1)S(1)}, bf16[4,3,32,256]{3,2,1,0:T(8,128)(2,1)S(1)}, u32[]{:S(2)}, u32[]{:S(2)}) %collective-permute-start.2) | collective-permute-done | bytes 196640 | tf_op jit(solution)/shard_map/ppermute | solution.py:31
  10.2 0.1 shard_map.101
  10.3 1.9 %collective-permute-start.4 = (bf16[3,14,32,256]{3,2,1,0:T(8,128)(2,1)S(1)}, bf16[3,14,32,256]{3,2,1,0:T(8,128)(2,1)S(1)}, u32[]{:S(2)}, u32[]{:S(2)}) collective-permute-start(bf16[3,14,32,256]{3,2,1,0:T(8,128)(2,1)S(1)} %get-tuple-element.32), channel_id=1, source_target_pairs={{0,4},{4,0},{8,12},{12,8},{16,20},{20,16},{24,28},{28,24},{1,5},{5... | collective-permute-start | bytes 2064392 | tf_op jit(solution)/shard_map/ppermute | solution.py:31
  12.1 3.0 %collective-permute-start = (bf16[3,8,32,256]{3,2,1,0:T(8,128)(2,1)S(1)}, bf16[3,8,32,256]{3,2,1,0:T(8,128)(2,1)S(1)}, u32[]{:S(2)}, u32[]{:S(2)}) collective-permute-start(bf16[3,8,32,256]{3,2,1,0:T(8,128)(2,1)S(1)} %get-tuple-element.27), channel_id=1, source_target_pairs={{4,8},{8,4},{12,16},{16,12},{20,24},{24,20},{5,9},{9,5},{13,17},{1... | collective-permute-start | bytes 1179656 | tf_op jit(solution)/shard_map/ppermute | solution.py:31
  15.2 3.1 %shard_map.102 = (bf16[192,768]{1,0:T(8,128)(2,1)S(1)}, bf16[192,768]{1,0:T(8,128)(2,1)S(1)}, bf16[160,672]{1,0:T(8,128)(2,1)S(1)}, bf16[96,480]{1,0:T(8,128)(2,...) custom-call(f32[1,32]{1,0:T(1,128)} %bitcast.6, ...), custom_call_target="tpu_custom_call" | custom-call | flops 2000000000 | bytes 2249600 | tf_op jit(solution)/shard_map/pallas_call | solution.py:36
  18.3 3.4 %collective-permute-start.3 = (bf16[3,6,32,256]{3,2,1,0:T(8,128)(2,1)S(1)}, bf16[3,6,32,256]{3,2,1,0:T(8,128)(2,1)S(1)}, u32[]{:S(2)}, u32[]{:S(2)}) collective-permute-start(bf16[3,6,32,256]{3,2,1,0:T(8,128)(2,1)S(1)} %get-tuple-element.31), channel_id=1, source_target_pairs={{4,8},{8,4},{12,16},{16,12},{20,24},{24,20},{5,9},{9,5},{13,17},{1... | collective-permute-start | bytes 884744 | tf_op jit(solution)/shard_map/ppermute | solution.py:31
  21.7 0.0 collective-permute-done.4.near
  21.7 4.6 %shard_map.103 = (f32[3,5,16,256]{3,2,1,0:T(8,128)S(1)}, bf16[3,2,14,32,256]{4,3,2,1,0:T(8,128)(2,1)S(1)}) custom-call(bf16[4,8,32,256]{3,2,1,0:T(8,128)(2,1)S(1)} %get-tuple-element.28.own_ref.own, bf16[3,14,32,256]{3,2,1,0:T(8,128)(2,1)S(1)} %collective-permute-done.4.near, bf16[4,3,32,256]{3,2,1,0:T(8,128)(2,1)S(1)} %collective-permute-done.1.even_ref.yeven, ...), custom_call_target="tpu_custom_call" | custom-call | flops 6000000000 | bytes 5328896 | tf_op jit(solution)/shard_map/pallas_call | solution.py:36
  26.3 0.0 collective-permute-done.far
  26.3 5.7 %collective-permute-done.3.corner = bf16[3,6,32,256]{3,2,1,0:T(8,128)(2,1)S(1)} collective-permute-done((bf16[3,6,32,256]{3,2,1,0:T(8,128)(2,1)S(1)}, bf16[3,6,32,256]{3,2,1,0:T(8,128)(2,1)S(1)}, u32[]{:S(2)}, u32[]{:S(2)}) %collective-permute-start.3) | collective-permute-done | bytes 294944 | tf_op jit(solution)/shard_map/ppermute | solution.py:31
  32.1 2.9 %shard_map.104 = f32[3,4,8,256]{3,2,1,0:T(8,128)} custom-call(bf16[3,8,32,256]{3,2,1,0:T(8,128)(2,1)S(1)} %collective-permute-done.far, bf16[3,6,32,256]{3,2,1,0:T(8,128)(2,1)S(1)} %collective-permute-done.3.corner, bf16[3,2,14,32,256]{4,3,2,1,0:T(8,128)(2,1)S(1)} %get-tuple-element.45.tail, f32[3,5,16,256]{3,2,1,0:T(8,128)S(1)} %get-tuple-element.46.mean, ...), custom_call_target="tpu_custom_call" | custom-call | flops 2000000000 | bytes 4374528 | tf_op jit(solution)/shard_map/pallas_call | solution.py:36
Async XLA Ops:
  0.0 1.0 %copy-start = (bf16[32,4,8,256]{3,2,1,0:T(8,128)(2,1)S(1)}, bf16[32,4,8,256]{3,2,1,0:T(8,128)(2,1)}, u32[]{:S(2)}) copy-start(bf16[32,4,8,256]{3,2,1,0:T(8,128)(2,1)} %feat_ref.1) | copy-start | bytes 1572868
  1.5 5.9 %collective-permute-start.1 = (bf16[4,3,32,256]{3,2,1,0:T(8,128)(2,1)S(1)}, bf16[4,3,32,256]{3,2,1,0:T(8,128)(2,1)S(1)}, u32[]{:S(2)}, u32[]{:S(2)}) collective-permute-start(bf16[4,3,32,256]{3,2,1,0:T(8,128)(2,1)S(1)} %get-tuple-element.29), channel_id=1, source_target_pairs={{0,1},{1,0},{2,3},{3,2},{4,5},{5,4},{6,7},{7,6},{8,9},{9,8},{10,11... | collective-permute-start | bytes 589832 | tf_op jit(solution)/shard_map/ppermute | solution.py:31
  2.8 7.4 %collective-permute-start.2 = (bf16[4,3,32,256]{3,2,1,0:T(8,128)(2,1)S(1)}, bf16[4,3,32,256]{3,2,1,0:T(8,128)(2,1)S(1)}, u32[]{:S(2)}, u32[]{:S(2)}) collective-permute-start(bf16[4,3,32,256]{3,2,1,0:T(8,128)(2,1)S(1)} %get-tuple-element.30), channel_id=1, source_target_pairs={{1,2},{2,1},{5,6},{6,5},{9,10},{10,9},{13,14},{14,13},{17,18},{18,... | collective-permute-start | bytes 589832 | tf_op jit(solution)/shard_map/ppermute | solution.py:31
  10.3 11.4 %collective-permute-start.4 = (bf16[3,14,32,256]{3,2,1,0:T(8,128)(2,1)S(1)}, bf16[3,14,32,256]{3,2,1,0:T(8,128)(2,1)S(1)}, u32[]{:S(2)}, u32[]{:S(2)}) collective-permute-start(bf16[3,14,32,256]{3,2,1,0:T(8,128)(2,1)S(1)} %get-tuple-element.32), channel_id=1, source_target_pairs={{0,4},{4,0},{8,12},{12,8},{16,20},{20,16},{24,28},{28,24},{1,5},{5... | collective-permute-start | bytes 2064392 | tf_op jit(solution)/shard_map/ppermute | solution.py:31
  12.1 14.2 %collective-permute-start = (bf16[3,8,32,256]{3,2,1,0:T(8,128)(2,1)S(1)}, bf16[3,8,32,256]{3,2,1,0:T(8,128)(2,1)S(1)}, u32[]{:S(2)}, u32[]{:S(2)}) collective-permute-start(bf16[3,8,32,256]{3,2,1,0:T(8,128)(2,1)S(1)} %get-tuple-element.27), channel_id=1, source_target_pairs={{4,8},{8,4},{12,16},{16,12},{20,24},{24,20},{5,9},{9,5},{13,17},{1... | collective-permute-start | bytes 1179656 | tf_op jit(solution)/shard_map/ppermute | solution.py:31
  18.3 13.8 %collective-permute-start.3 = (bf16[3,6,32,256]{3,2,1,0:T(8,128)(2,1)S(1)}, bf16[3,6,32,256]{3,2,1,0:T(8,128)(2,1)S(1)}, u32[]{:S(2)}, u32[]{:S(2)}) collective-permute-start(bf16[3,6,32,256]{3,2,1,0:T(8,128)(2,1)S(1)} %get-tuple-element.31), channel_id=1, source_target_pairs={{4,8},{8,4},{12,16},{16,12},{20,24},{24,20},{5,9},{9,5},{13,17},{1... | collective-permute-start | bytes 884744 | tf_op jit(solution)/shard_map/ppermute | solution.py:31

commit v2 on v1

--- a/solution.py
+++ b/solution.py
@@ -11,6 +11,7 @@
 HALO = 3
 SPAN = 6
 WIDE = SPAN + 2
+EDGE = 3
 F32, BF16 = jnp.float32, jnp.bfloat16
 VMEM = pl.BlockSpec(memory_space=pltpu.VMEM)
 HBM = pl.BlockSpec(memory_space=pltpu.HBM)
@@ -48,38 +49,34 @@
     return lax.rem(lax.axis_index(axis), 2)
 
 
-def pack_kernel(feat_ref, own_ref, far_ref, even_ref, odd_ref):
+def cell_order(channels, rows):
+    size = channels * rows
+    row, col = iota((size, size), 0), iota((size, size), 1)
+    return ((row // channels == col % rows) & (row % channels == col // rows)).astype(F32).astype(BF16)
+
+
+def pack_kernel(feat_ref, own_ref, even_ref, odd_ref, far_ref):
     channels, depth, rows, cols = feat_ref.shape
     size = channels * rows
-    row, col = iota((size, size), 0), iota((size, size), 1)
-    order = ((row // channels == col % rows) & (row % channels == col // rows)).astype(F32).astype(BF16)
+    order = cell_order(channels, rows)
     part_z, part_y = odd("gz"), odd("gy")
     for z in range(depth):
         value = feat_ref[:, z].astype(F32).reshape(size, cols).astype(BF16)
         value = matmul(order, value).astype(BF16).reshape(rows, channels, cols)
         own_ref[part_z * z + (1 - part_z) * (depth - 1 - z)] = value
     first_even, first_odd = (1 - part_y) * (rows - HALO), part_y * (rows - HALO)
-    for layer in range(HALO):
-        far_ref[layer] = own_ref[depth - 1 - layer]
     for z in range(depth):
         for row in range(HALO):
             even_ref[z, row] = own_ref[z, first_even + row]
             odd_ref[z, row] = own_ref[z, first_odd + row]
-
-
-def rim_kernel(own_ref, even_ref, odd_ref, near_ref, corner_ref):
-    depth, rows = own_ref.shape[:2]
     for layer in range(HALO):
-        near_ref[layer, :rows] = own_ref[layer]
-        near_ref[layer, rows : rows + HALO] = even_ref[layer]
-        near_ref[layer, rows + HALO :] = odd_ref[layer]
-        corner_ref[layer, :HALO] = even_ref[depth - 1 - layer]
-        corner_ref[layer, HALO:] = odd_ref[depth - 1 - layer]
+        far_ref[layer] = own_ref[depth - 1 - layer]
 
 
 def weights_kernel(
     scale1_hbm, shift1_hbm, conv1_hbm, bias1_hbm, scale2_hbm, shift2_hbm, conv2_hbm, bias2_hbm, flow_hbm,
-    wxy_ref, wyz_ref, wza_ref, wzb_ref, vxy_ref, vyz_ref, vza_ref, vzb_ref, vf_ref,
+    wxy_ref, wyz_ref, wza_ref, wzb_ref, wxe_ref, wye_ref,
+    vxy_ref, vyz_ref, vza_ref, vzb_ref, vxe_ref, vye_ref, vf_ref,
     s1_ref, t1_ref, s2_ref, t2_ref, const_ref,
     scale1, shift1, conv1, bias1, scale2, shift2, conv2, bias2, flow, taps, folds, sem,
 ):
@@ -146,11 +143,13 @@
     banded(wyz_ref, lambda g, i: taps[along_z(g), i])
     banded(wza_ref, lambda g, i: taps[along_z(i), g])
     banded(wzb_ref, lambda g, i: taps[along_z(i), g])
-
-    def banded_flow(ref, pick, skip):
+    banded(wxe_ref, lambda g, i: taps[i, g])
+    banded(wye_ref, lambda g, i: taps[along_z(g), i])
+
+    def banded_flow(ref, pick, place):
         cols = ref.shape[1]
         height = ref.shape[0] // 12
-        band = iota((height, cols), 1) // c + skip - iota((height, cols), 0)
+        band = place(iota((height, cols), 1) // c) - iota((height, cols), 0)
         for part in range(2):
             for g in range(3):
                 for k in range(2):
@@ -161,10 +160,14 @@
                     at = ((part * 3 + g) * 2 + k) * height
                     ref[at : at + height] = block.astype(BF16)
 
-    banded_flow(vxy_ref, lambda g, i: (i, g), 0)
-    banded_flow(vyz_ref, lambda g, i: (along_z(g), i), 0)
-    banded_flow(vza_ref, lambda g, i: (along_z(i), g), 0)
-    banded_flow(vzb_ref, lambda g, i: (along_z(i), g), vza_ref.shape[1] // c)
+    middle = vxy_ref.shape[1] // c - 2 * EDGE
+    past = vza_ref.shape[1] // c
+    banded_flow(vxy_ref, lambda g, i: (i, g), lambda b: b)
+    banded_flow(vyz_ref, lambda g, i: (along_z(g), i), lambda b: b)
+    banded_flow(vza_ref, lambda g, i: (along_z(i), g), lambda b: b)
+    banded_flow(vzb_ref, lambda g, i: (along_z(i), g), lambda b: b + past)
+    banded_flow(vxe_ref, lambda g, i: (i, g), lambda b: jnp.where(b < EDGE, b, b + middle))
+    banded_flow(vye_ref, lambda g, i: (along_z(g), i), lambda b: jnp.where(b < EDGE, b, b + middle))
     cols = vf_ref.shape[1]
     plain = matmul(flow[...], short)
     for k in range(2):
@@ -173,12 +176,12 @@
 
 
 def shift_right(value):
-    return jnp.where(iota(value.shape, 1) == 0, 0.0, pltpu.roll(value, 1, 1))
+    return jnp.where(iota(value.shape, 1) == 0, jnp.zeros_like(value), pltpu.roll(value, 1, 1))
 
 
 def shift_left(value):
     last = value.shape[1] - 1
-    return jnp.where(iota(value.shape, 1) == last, 0.0, pltpu.roll(value, last, 1))
+    return jnp.where(iota(value.shape, 1) == last, jnp.zeros_like(value), pltpu.roll(value, last, 1))
 
 
 def valid_sides():
@@ -205,7 +208,8 @@
     value = jnp.maximum(value.reshape(size, cols).astype(F32) * s1[:size] + t1[:size], 0.0)
     if valid is not None:
         value = value * valid
-    return [v.astype(BF16).reshape(count, c, cols) for v in (shift_right(value), value, shift_left(value))]
+    value = value.astype(BF16)
+    return [v.reshape(count, c, cols) for v in (shift_right(value), value, shift_left(value))]
 
 
 def set_masks(sm, tm, s2, t2, low_y, high_y):
@@ -240,45 +244,21 @@
     return shift_right(value[:step]) + value[step : 2 * step] + shift_left(value[2 * step :])
 
 
-def planes(
-    unit, xy_layers, out_layers, out_xz, data_xz, edge_xz,
-    wxy, wyz, wz, vxy, vyz, vz, s2, t2, sm, tm, act_xy, act_yz, act_xz, fxz, outer,
-):
-    c, cols = act_xy.shape[-2:]
-    wide = act_xy.shape[1]
-    flow_xy, flow_yz = {}, {}
-    for n, z in enumerate(xy_layers):
-        for w in range(wide // SPAN):
-            data = stack([unit(j, z, slice(w * SPAN, w * SPAN + WIDE)) for j in range(3)])
-            act_xy[n, w * SPAN : (w + 1) * SPAN] = activate(matmul(wxy[...], data), sm[w], tm[w], c)
-    for n, z in enumerate(out_layers):
-        for w in range(wide // SPAN):
-            data = stack([unit(1, z + i - 1, slice(w * SPAN, w * SPAN + WIDE)) for i in range(3)])
-            act_yz[n, w * SPAN : (w + 1) * SPAN] = activate(matmul(wyz[...], data), sm[w], tm[w], c, outer(z))
-    count = len(out_xz)
-    row = iota((count * c, cols), 0)
-    keep = jnp.where((row >= edge_xz[0] * c) & (row < edge_xz[1] * c), edge_xz[2], 1.0)
-    scale, shift = s2[: count * c] * keep, t2[: count * c] * keep
-    for y in range(act_xz.shape[0]):
-        data = stack([unit(j, z, y + 2) for j in range(3) for z in data_xz])
-        act_xz[y] = activate(matmul(wz[...], data), scale, shift, c)
-    for y in range(act_xz.shape[0]):
-        flow = along_x(matmul(vz[...], act_xz[y].reshape(-1, cols)))
-        half = flow.shape[0] // 2
-        for k in range(2):
-            fxz[k, :, y, :] = flow[k * half : (k + 1) * half]
-    for n, z in enumerate(xy_layers):
-        flow_xy[z] = along_x(matmul(vxy[...], act_xy[n].reshape(-1, cols)))
-    for n, z in enumerate(out_layers):
-        value = two_parts(matmul(vyz[...], act_yz[n].reshape(-1, cols)))
-        step = value.shape[0] // 3
-        flow_yz[z] = [value[i * step : (i + 1) * step] for i in range(3)]
-    return flow_xy, flow_yz
-
-
-def gather_mean(add, layer, fxz, flow_xy, flow_yz, base, height):
-    at = layer - 2
-    parts = [0.5 * fxz[0, at], None, 0.5 * fxz[1, at]]
+def edge_scale(s2, count, first, valid):
+    c = s2.shape[0] // SPAN
+    row = iota((count * c, s2.shape[1]), 0)
+    keep = (row >= first * c) if first > 0 else (row < (count + first) * c)
+    return jnp.where(keep, 1.0, valid)
+
+
+def yz_parts(weights, cells):
+    value = two_parts(matmul(weights[...], cells))
+    step = value.shape[0] // 3
+    return [value[i * step : (i + 1) * step] for i in range(3)]
+
+
+def layer_parts(layer, flow_xz, flow_xy, flow_yz, base, height):
+    parts = [0.5 * flow_xz[0], None, 0.5 * flow_xz[1]]
 
     def plus(k, value):
         parts[k] = value if parts[k] is None else parts[k] + value
@@ -296,19 +276,71 @@
         plus(0, base[:height])
         plus(1, 0.5 * (base[:height] + base[height:]))
         plus(2, base[height:])
+    return parts
+
+
+def rim_kernel(
+    own, yeven, yodd, wye, wzb, vye, vza, s1, t1, s2, t2, near_ref, corner_ref, unit, part,
+):
+    depth, rows, c, cols = own.shape
+    for layer in range(HALO):
+        near_ref[layer, :rows] = own[layer]
+        near_ref[layer, rows : rows + HALO] = yeven[layer]
+        near_ref[layer, rows + HALO :] = yodd[layer]
+    for layer in range(2):
+        for row in range(HALO):
+            corner_ref[layer * 2 * HALO + row] = yeven[depth - 1 - layer, row]
+            corner_ref[layer * 2 * HALO + HALO + row] = yodd[depth - 1 - layer, row]
+
+    _, _, low_y, high_y = valid_sides()
+    (at_even, valid_even), (at_odd, valid_odd) = y_halos(rows, low_y, high_y)
+
+    def place(value, z, y, valid):
+        for j, moved in enumerate(normalized(value, s1, t1, valid)):
+            unit[j, z, pl.ds(y, value.shape[0])] = moved
+
+    for z in range(3):
+        layer = depth - 3 + z
+        place(own[layer, :2], z, HALO, None)
+        place(own[layer, rows - 2 :], z, HALO + rows - 2, None)
+        place(yeven[layer], z, at_even, valid_even)
+        place(yodd[layer], z, at_odd, valid_odd)
+    keeps = (edge_scale(s2, EDGE, 2, low_y), edge_scale(s2, EDGE, -2, high_y))
+    cells = []
+    for keep, window in zip(keeps, (range(EDGE + 2), range(rows + 1, rows + 6))):
+        data = stack([unit[1, i, y] for i in range(3) for y in window])
+        cells.append(activate(matmul(wye[...], data), s2[: EDGE * c] * keep, t2[: EDGE * c] * keep, c))
+    none = jnp.zeros((2 * c, cols), BF16)
+    ends = []
+    for at in (0, rows + 1):
+        data = stack([p for j in range(3) for p in (none, *(unit[j, z, at + 2] for z in range(3)))])
+        ends.append(activate(matmul(wzb[...], data)[2 * c :], s2[:c], t2[:c], c))
+    flow = yz_parts(vye, stack(cells))[0]
+    ends = [along_x(matmul(vza[...], stack([none, none, cell]))) for cell in ends]
+    height = part.shape[1]
+    part[0] = 0.5 * flow[:height]
+    part[1] = 0.5 * flow[height:]
+    part[2] = jnp.zeros((height, cols), F32)
+    for at, flow in zip((0, rows + 1), ends):
+        step = flow.shape[0] // 2
+        part[0, at : at + 1] = part[0, at : at + 1] + 0.5 * flow[depth : depth + 1]
+        part[2, at : at + 1] = 0.5 * flow[step + depth : step + depth + 1]
     for k in range(3):
-        if parts[k] is not None:
-            add(k, at, parts[k])
+        value = part[k]
+        top = value.astype(BF16)
+        corner_ref[4 * HALO + k, :height] = top
+        corner_ref[4 * HALO + k, height:] = (value - top.astype(F32)).astype(BF16)
 
 
 def near_kernel(
-    own, near, yeven, yodd, wxy, wyz, wz, vxy, vyz, vz, vf, s1, t1, s2, t2, const,
+    own, near, yeven, yodd, wxy, wyz, wza, vxy, vyz, vza, vf, s1, t1, s2, t2, const,
     mean, tail, unit, feat, act_xy, act_yz, act_xz, sm, tm, fxz,
 ):
-    depth, rows, _, cols = own.shape
+    depth, rows, c, cols = own.shape
     valid_near, _, low_y, high_y = valid_sides()
     (at_even, valid_even), (at_odd, valid_odd) = y_halos(rows, low_y, high_y)
-    first = HALO + depth - 2
+    start = HALO + depth
+    first = start - 2
 
     def place(value, z, y, valid):
         count = value.shape[0]
@@ -333,27 +365,93 @@
     def read(j, z, y):
         return unit[j, z, y] if z < first else tail[j, z - first, y]
 
-    outs = list(range(1, depth + 2))
-    flow_xy, flow_yz = planes(
-        read, list(range(2, depth + 3)), outs, outs, list(range(depth + 3)), (0, 2, valid_near),
-        wxy, wyz, wz, vxy, vyz, vz, s2, t2, sm, tm, act_xy, act_yz, act_xz, fxz,
-        lambda z: valid_near if z < HALO else None,
-    )
+    wide = rows + 4
+    for n, z in enumerate(range(2, start)):
+        for w in range(wide // SPAN):
+            data = stack([read(j, z, slice(w * SPAN, w * SPAN + WIDE)) for j in range(3)])
+            act_xy[n, w * SPAN : (w + 1) * SPAN] = activate(matmul(wxy[...], data), sm[w], tm[w], c)
+    for n, z in enumerate(range(1, first + 1)):
+        valid = valid_near if z < HALO else None
+        for w in range(wide // SPAN):
+            data = stack([read(1, z + i - 1, slice(w * SPAN, w * SPAN + WIDE)) for i in range(3)])
+            act_yz[n, w * SPAN : (w + 1) * SPAN] = activate(matmul(wyz[...], data), sm[w], tm[w], c, valid)
+    count = depth + 1
+    keep = edge_scale(s2, count, 2, valid_near)
+    scale, shift = s2[: count * c] * keep, t2[: count * c] * keep
+    for y in range(rows + 2):
+        data = stack([read(j, z, y + 2) for j in range(3) for z in range(depth + 3)])
+        act_xz[y] = activate(matmul(wza[...], data), scale, shift, c)
+    for y in range(rows + 2):
+        flow = along_x(matmul(vza[...], act_xz[y].reshape(-1, cols)))
+        half = flow.shape[0] // 2
+        for k in range(2):
+            fxz[k, :, y, :] = flow[k * half : (k + 1) * half]
     height = mean.shape[2]
-
-    def store(k, at, value):
-        mean[k, at] = value
-
-    for layer in range(2, depth + 3):
-        base = matmul(vf[...], feat[layer - 2, 2 : rows + 4].reshape(-1, cols)) + const[...]
-        gather_mean(store, layer, fxz, flow_xy, flow_yz, base, height)
+    flow_xy = {z: along_x(matmul(vxy[...], act_xy[n].reshape(-1, cols))) for n, z in enumerate(range(2, start))}
+    flow_yz = {z: yz_parts(vyz, act_yz[n].reshape(-1, cols)) for n, z in enumerate(range(1, first + 1))}
+    for layer in range(2, start):
+        at = layer - 2
+        base = matmul(vf[...], feat[at, 2 : rows + 4].reshape(-1, cols)) + const[...]
+        for k, value in enumerate(layer_parts(layer, (fxz[0, at], fxz[1, at]), flow_xy, flow_yz, base, height)):
+            mean[k, at] = value
+
+
+def mid_kernel(
+    last, far, tail, wxy, wyz, wzb, vxy, vyz, vzb, vf, s1, t1, s2, t2, const,
+    more, face, fxz,
+):
+    _, rows, c, cols = far.shape
+    _, valid_far, _, _ = valid_sides()
+    for z in range(HALO):
+        for j, moved in enumerate(normalized(far[z], s1, t1, valid_far)):
+            face[j, z] = moved
+
+    def read(j, z, y):
+        return tail[j, z, y + HALO] if z < 2 else face[j, z - 2, y]
+
+    keep = edge_scale(s2, EDGE, -2, valid_far)
+    scale, shift = s2[: EDGE * c] * keep, t2[: EDGE * c] * keep
+    gap = jnp.zeros((EDGE * c, cols), BF16)
+
+    def middle(cells):
+        return jnp.concatenate([gap, cells.reshape(-1, cols), gap], axis=0)
+
+    inner = slice(HALO, HALO + rows)
+    data = stack([face[j, 0] for j in range(3)])
+    act_xy = activate(matmul(wxy[...], data), s2[...], t2[...], c)
+    act_yz = []
+    for z in range(1, 4):
+        data = stack([tail[1, i, inner] if i < 2 else face[1, i - 2] for i in range(z - 1, z + 2)])
+        act_yz.append(activate(matmul(wyz[...], data), s2[...], t2[...], c, valid_far if z > 1 else None))
+    act_xz = []
+    for y in range(rows):
+        data = stack([read(j, z, y) for j in range(3) for z in range(EDGE + 2)])
+        act_xz.append(activate(matmul(wzb[...], data), scale, shift, c))
+    flow_xy = {2: along_x(matmul(vxy[...], middle(act_xy)))}
+    flow_yz = {z: yz_parts(vyz, middle(act_yz[z - 1])) for z in range(1, 4)}
+    flow_xz = [along_x(matmul(vzb[...], cells.reshape(-1, cols))) for cells in act_xz]
+    fxz[...] = jnp.zeros_like(fxz)
+    for y, flow in enumerate(flow_xz):
+        half = flow.shape[0] // 2
+        for k in range(2):
+            fxz[k, :, y + 1, :] = flow[k * half : (k + 1) * half]
+    height = more.shape[2]
+    for layer in range(3):
+        base = None
+        if layer == 2:
+            cells = jnp.concatenate([gap[:c], far[0].reshape(-1, cols), gap[:c]], axis=0)
+            base = matmul(vf[...], cells) + const[...]
+        at = last + layer - 2
+        for k, value in enumerate(layer_parts(layer, (fxz[0, at], fxz[1, at]), flow_xy, flow_yz, base, height)):
+            more[k, layer] = value
 
 
 def far_kernel(
-    far, corner, tail, mean, wxy, wyz, wz, vxy, vyz, vz, vf, s1, t1, s2, t2, const,
-    out, unit, act_xy, act_yz, act_xz, sm, tm, fxz, feat, total,
+    corner, tail, face, mean, more, wzb, wxe, wye, vzb, vxe, vye, vf, s1, t1, s2, t2,
+    out, unit, fxz, feat, total,
 ):
     _, depth, rows, cols = out.shape
+    c = corner.shape[1]
     valid_near, valid_far, low_y, high_y = valid_sides()
     (at_even, valid_even), (at_odd, valid_odd) = y_halos(rows, low_y, high_y)
     start = HALO + depth
@@ -366,38 +464,68 @@
         for j, moved in enumerate(normalized(value, s1, t1, valid)):
             unit[j, z, pl.ds(y, count)] = moved
 
-    for z in range(HALO):
-        place(far[z], z, HALO, valid_far)
-        place(corner[z, :HALO], z, at_even, valid_far * valid_even)
-        place(corner[z, HALO:], z, at_odd, valid_far * valid_odd)
-    set_masks(sm, tm, s2, t2, low_y, high_y)
+    for z in range(2):
+        at = z * 2 * HALO
+        place(corner[at : at + HALO], z, at_even, valid_far * valid_even)
+        place(corner[at + HALO : at + 2 * HALO], z, at_odd, valid_far * valid_odd)
 
     def read(j, z, y):
-        return unit[j, z - start, y] if z >= start else tail[j, z - first, y]
-
-    outs = list(range(start - 1, start + 2))
-    flow_xy, flow_yz = planes(
-        read, [start], outs, outs, list(range(first, start + HALO)), (1, 3, valid_far),
-        wxy, wyz, wz, vxy, vyz, vz, s2, t2, sm, tm, act_xy, act_yz, act_xz, fxz,
-        lambda z: valid_far if z >= start else None,
-    )
+        if z < start:
+            return tail[j, z - first, y]
+        return face[j, z - start, y - HALO] if HALO <= y < HALO + rows else unit[j, z - start, y]
+
+    low, high = range(EDGE + 2), range(rows + 1, rows + 6)
+    keeps = (edge_scale(s2, EDGE, 2, low_y), edge_scale(s2, EDGE, -2, high_y))
+    scales = [s2[: EDGE * c] * keep for keep in keeps]
+    shifts = [t2[: EDGE * c] * keep for keep in keeps]
+    keep = edge_scale(s2, 2, -1, valid_far)
+    scale, shift = s2[: 2 * c] * keep, t2[: 2 * c] * keep
+    none = jnp.zeros((c, cols), BF16)
+    act_xy = []
+    for side, window in enumerate((low, high)):
+        data = stack([read(j, start, y) for j in range(3) for y in window])
+        act_xy.append(activate(matmul(wxe[...], data), scales[side], shifts[side], c))
+    act_yz = {}
+    for z in range(first + 1, start + 1):
+        for side, window in enumerate((low, high)):
+            data = stack([read(1, z + i - 1, y) for i in range(3) for y in window])
+            valid = valid_far if z >= start else None
+            act_yz[z, side] = activate(matmul(wye[...], data), scales[side], shifts[side], c, valid)
+    act_xz = []
+    for y in (0, rows + 1):
+        data = stack([p for j in range(3) for p in (*(read(j, first + z, y + 2) for z in range(4)), none)])
+        act_xz.append(activate(matmul(wzb[...], data)[: 2 * c], scale, shift, c))
+    flow_xy = {start: along_x(matmul(vxe[...], stack(act_xy)))}
+    flow_yz = {z: yz_parts(vye, stack([act_yz[z, 0], act_yz[z, 1]])) for z in range(first + 1, start + 1)}
+    flow_xz = [along_x(matmul(vzb[...], stack([cells, none]))) for cells in act_xz]
+    fxz[...] = jnp.zeros_like(fxz)
+    for y, flow in zip((0, rows + 1), flow_xz):
+        half = flow.shape[0] // 2
+        for k in range(2):
+            fxz[k, :, y, :] = flow[k * half : (k + 1) * half]
+    gap = jnp.zeros((rows * c, cols), BF16)
+    base = matmul(vf[...], jnp.concatenate([feat[2], gap, feat[rows + 3]], axis=0))
+
     height = mean.shape[2]
     spot = iota((height, cols), 0)
     inside_y = jnp.where(spot == 0, low_y, jnp.where(spot == rows + 1, high_y, jnp.where(spot < rows + 1, 1.0, 0.0)))
-
-    def store(k, at, value):
-        if at < depth + 1:
-            value = value + mean[k, at]
-        total[k, at] = value * (inside_y * valid_far if at == depth + 1 else inside_y)
-
-    for k in range(3):
-        for at in range(depth - 1):
-            total[k, at] = mean[k, at] * (inside_y * valid_near if at == 0 else inside_y)
-    for layer in range(first, start + 1):
-        base = None
-        if layer == start:
-            base = matmul(vf[...], feat[2 : rows + 4].reshape(-1, cols)) + const[...]
-        gather_mean(store, layer, fxz, flow_xy, flow_yz, base, height)
+    for layer in range(2, start + 1):
+        at = layer - 2
+        keep = inside_y * valid_near if at == 0 else inside_y * valid_far if layer == start else inside_y
+        if layer < first:
+            for k in range(3):
+                total[k, at] = mean[k, at] * keep
+        else:
+            added = layer_parts(
+                layer, (fxz[0, at], fxz[1, at]), flow_xy, flow_yz, base if layer == start else None, height
+            )
+            for k in range(3):
+                value = more[k, layer - first] + added[k]
+                if layer < start:
+                    value = value + mean[k, at]
+                else:
+                    value = value + corner[4 * HALO + k, :height].astype(F32) + corner[4 * HALO + k, height:].astype(F32)
+                total[k, at] = value * keep
     part_z = odd("gz")
     for k in range(3):
         for z in range(depth):
@@ -415,14 +543,14 @@
     shape = jax.ShapeDtypeStruct
     cells = functools.partial(shape, dtype=BF16)
     side = cells((depth, HALO, c, cols))
-    own, send_far, send_even, send_odd = call(
+    own, send_even, send_odd, send_far = call(
         pack_kernel,
-        [cells((depth, rows, c, cols)), cells((HALO, rows, c, cols)), side, side],
+        [cells((depth, rows, c, cols)), side, side, cells((HALO, rows, c, cols))],
         [features], 2 * features.size * c * rows, 6,
     )
-    far = swap(send_far, "gz", 1)
     yeven = swap(send_even, "gy", 0)
     yodd = swap(send_odd, "gy", 1)
+    far = swap(send_far, "gz", 1)
 
     broad = rows + 2 * HALO
     high = -(-(rows + 2) // 8) * 8
@@ -432,17 +560,18 @@
         scale_second[None], shift_second[None], conv_second, bias_second[None], flow_weight,
     ]
     params = [pltpu.with_memory_space_constraint(p, pltpu.HBM) for p in params]
-    wxy, wyz, wza, wzb, vxy, vyz, vza, vzb, *rest = call(
+    wxy, wyz, wza, wzb, wxe, wye, vxy, vyz, vza, vzb, vxe, vye, vf, *rest = call(
         weights_kernel,
         [
             cells((SPAN * c, 3 * WIDE * c)),
             cells((SPAN * c, 3 * WIDE * c)),
             cells(((depth + 1) * c, 3 * (depth + 3) * c)),
-            cells((HALO * c, 3 * (HALO + 2) * c)),
+            *[cells((EDGE * c, 3 * (EDGE + 2) * c))] * 3,
             cells((12 * high, (rows + 4) * c)),
             cells((12 * high, (rows + 4) * c)),
             cells((12 * deep, (depth + 1) * c)),
-            cells((12 * deep, HALO * c)),
+            cells((12 * deep, EDGE * c)),
+            *[cells((12 * high, 2 * EDGE * c))] * 2,
             cells((2 * high, (rows + 2) * c)),
             shape((rows * c, cols), F32),
             shape((rows * c, cols), F32),
@@ -460,43 +589,48 @@
         ],
         HBM,
     )
+    assert c == 2 * high
     send_near, send_corner = call(
         rim_kernel,
-        [cells((HALO, broad, c, cols)), cells((HALO, 2 * HALO, c, cols))],
-        [own, yeven, yodd], 10**6, 5,
+        [cells((HALO, broad, c, cols)), cells((4 * HALO + 3, c, cols))],
+        [own, yeven, yodd, wye, wzb, vye, vza, *rest[:4]],
+        10**8, 10,
+        [pltpu.VMEM((3, 3, broad, c, cols), BF16), pltpu.VMEM((3, high, cols), F32)],
     )
     corner = swap(send_corner, "gz", 1)
     near = swap(send_near, "gz", 0)
 
-    def scratch(layers_xy, layers_out):
-        return [
-            pltpu.VMEM((layers_xy, rows + 4, c, cols), BF16),
-            pltpu.VMEM((layers_out, rows + 4, c, cols), BF16),
-            pltpu.VMEM((rows + 2, layers_out, c, cols), BF16),
-            pltpu.VMEM((2, SPAN * c, cols), F32),
-            pltpu.VMEM((2, SPAN * c, cols), F32),
-            pltpu.VMEM((2, deep, high, cols), F32),
-        ]
-
     mean, tail = call(
         near_kernel,
         [shape((3, depth + 1, high, cols), F32), cells((3, 2, broad, c, cols))],
-        [own, near, yeven, yodd, wxy, wyz, wza, vxy, vyz, vza, *rest],
+        [own, near, yeven, yodd, wxy, wyz, wza, vxy, vyz, vza, vf, *rest],
         6 * 10**9, 24,
         [
             pltpu.VMEM((3, depth + 1, broad, c, cols), BF16),
             pltpu.VMEM((depth + 1, broad, c, cols), BF16),
-            *scratch(depth + 1, depth + 1),
+            pltpu.VMEM((depth + 1, rows + 4, c, cols), BF16),
+            pltpu.VMEM((depth + 1, rows + 4, c, cols), BF16),
+            pltpu.VMEM((rows + 2, depth + 1, c, cols), BF16),
+            pltpu.VMEM((2, SPAN * c, cols), F32),
+            pltpu.VMEM((2, SPAN * c, cols), F32),
+            pltpu.VMEM((2, deep, high, cols), F32),
         ],
+    )
+    more, face = call(
+        functools.partial(mid_kernel, depth + 1),
+        [shape((3, 3, high, cols), F32), cells((3, HALO, rows, c, cols))],
+        [far, tail, wxy, wyz, wzb, vxy, vyz, vzb, vf, *rest],
+        3 * 10**9, 12,
+        [pltpu.VMEM((2, deep, high, cols), F32)],
     )
     (out,) = call(
         far_kernel,
         [shape((3, depth, rows, cols), F32)],
-        [far, corner, tail, mean, wxy, wyz, wzb, vxy, vyz, vzb, *rest],
+        [corner, tail, face, mean, more, wzb, wxe, wye, vzb, vxe, vye, vf, *rest[:4]],
         2 * 10**9, 16,
         [
             pltpu.VMEM((3, HALO, broad, c, cols), BF16),
-            *scratch(1, HALO),
+            pltpu.VMEM((2, deep, high, cols), F32),
             pltpu.VMEM((broad, c, cols), BF16),
             pltpu.VMEM((3, depth + 2, high, cols), F32),
         ],

time: 35.2 us -> 33.6 us (0.955)
  waiting for transfers between devices: 11.2 us -> 8.72 us
  Pallas kernels: 11 us -> 12 us
    ppermute x5, waiting for transfers between devices: 11.2 us -> 8.72 us  [swap(): return lax.ppermute(value, axis, pairs)]
    pallas_call x5 -> x6, Pallas kernels: 11 us -> 12 us  [call(): pl.pallas_call(kernel, out_shape=outs, in_specs=[space] * len(args), out_...]
  transfers between devices with their start and end apart: 5 -> 5, of which waited for: 3 -> 3; matrix products, arithmetic and copies ran while one was open for 0% -> 0% of each run, Pallas kernels for 22% -> 27%
where the time goes in v2:
time: 33.6 us; the launch traced here: 33.4 us
  Pallas kernels  12 us (36%)
  starting transfers between devices  11.6 us (35%)
  waiting for transfers between devices  8.72 us (26%)
  local copies, waits for them, and re-layouts  1.04 us (3%)
    pallas_call x6, Pallas kernels, call(): pl.pallas_call(kernel, out_shape=outs, in_specs=[space] * len(args), out_...  12 us
    ppermute x5, starting transfers between devices, swap(): return lax.ppermute(value, axis, pairs)  11.6 us
    ppermute x5, waiting for transfers between devices, swap(): return lax.ppermute(value, axis, pairs)  8.72 us
    unnamed x2, local copies, waits for them, and re-layouts  1.04 us
  transfers between devices with their start and end apart: 5, of which 3 were waited for; matrix products, arithmetic and copies ran while one was open for 0% of the time, Pallas kernels for 27%

profile of v2, /device:TPU:19, one launch (start us, length us, event | category | flops | bytes accessed | tf_op | source)
XLA Modules:
  0.0 33.4 jit_solution(3555081152502804516)
XLA Ops:
  0.0 0.0 copy-start
  0.0 1.0 %copy-done = bf16[32,4,8,256]{3,2,1,0:T(8,128)(2,1)S(1)} copy-done((bf16[32,4,8,256]{3,2,1,0:T(8,128)(2,1)S(1)}, bf16[32,4,8,256]{3,2,1,0:T(8,128)(2,1)}, u32[]{:S(2)}) %copy-start) | copy-done | bytes 524312
  1.0 0.4 %shard_map.100 = (bf16[4,8,32,256]{3,2,1,0:T(8,128)(2,1)S(1)}, bf16[4,3,32,256]{3,2,1,0:T(8,128)(2,1)S(1)}, bf16[4,3,32,256]{3,2,1,0:T(8,128)(2,1)S(1)}, bf16[3,8,32,256]{3,2,1,0:T(8,128)(2,1)S(1)}) custom-call(bf16[32,4,8,256]{3,2,1,0:T(8,128)(2,1)S(1)} %copy-done), custom_call_target="tpu_custom_call" | custom-call | flops 134217728 | bytes 1835008 | tf_op jit(solution)/shard_map/pallas_call | solution.py:37
  1.5 1.4 %collective-permute-start = (bf16[4,3,32,256]{3,2,1,0:T(8,128)(2,1)S(1)}, bf16[4,3,32,256]{3,2,1,0:T(8,128)(2,1)S(1)}, u32[]{:S(2)}, u32[]{:S(2)}) collective-permute-start(bf16[4,3,32,256]{3,2,1,0:T(8,128)(2,1)S(1)} %get-tuple-element.34), channel_id=1, source_target_pairs={{0,1},{1,0},{2,3},{3,2},{4,5},{5,4},{6,7},{7,6},{8,9},{9,8},{10,11... | collective-permute-start | bytes 589832 | tf_op jit(solution)/shard_map/ppermute | solution.py:32
  2.8 1.9 %collective-permute-start.1 = (bf16[4,3,32,256]{3,2,1,0:T(8,128)(2,1)S(1)}, bf16[4,3,32,256]{3,2,1,0:T(8,128)(2,1)S(1)}, u32[]{:S(2)}, u32[]{:S(2)}) collective-permute-start(bf16[4,3,32,256]{3,2,1,0:T(8,128)(2,1)S(1)} %get-tuple-element.35), channel_id=1, source_target_pairs={{1,2},{2,1},{5,6},{6,5},{9,10},{10,9},{13,14},{14,13},{17,18},{18,... | collective-permute-start | bytes 589832 | tf_op jit(solution)/shard_map/ppermute | solution.py:32
  4.7 3.3 %shard_map.101 = (bf16[192,768]{1,0:T(8,128)(2,1)S(1)}, bf16[192,768]{1,0:T(8,128)(2,1)S(1)}, bf16[160,672]{1,0:T(8,128)(2,1)S(1)}, bf16[96,480]{1,0:T(8,128)(2,...) custom-call(f32[1,32]{1,0:T(1,128)} %bitcast.6, ...), custom_call_target="tpu_custom_call" | custom-call | flops 2000000000 | bytes 2581376 | tf_op jit(solution)/shard_map/pallas_call | solution.py:37
  8.1 0.0 collective-permute-done.yeven
  8.1 2.1 %collective-permute-done.1.yodd = bf16[4,3,32,256]{3,2,1,0:T(8,128)(2,1)S(1)} collective-permute-done((bf16[4,3,32,256]{3,2,1,0:T(8,128)(2,1)S(1)}, bf16[4,3,32,256]{3,2,1,0:T(8,128)(2,1)S(1)}, u32[]{:S(2)}, u32[]{:S(2)}) %collective-permute-start.1) | collective-permute-done | bytes 196640 | tf_op jit(solution)/shard_map/ppermute | solution.py:32
  10.2 0.8 %shard_map.102 = (bf16[3,14,32,256]{3,2,1,0:T(8,128)(2,1)S(1)}, bf16[15,32,256]{2,1,0:T(8,128)(2,1)S(1)}) custom-call(bf16[4,8,32,256]{3,2,1,0:T(8,128)(2,1)S(1)} %get-tuple-element.33.own, bf16[4,3,32,256]{3,2,1,0:T(8,128)(2,1)S(1)} %collective-permute-done.yeven, bf16[4,3,32,256]{3,2,1,0:T(8,128)(2,1)S(1)} %collective-permute-done.1.yodd, ...), custom_call_target="tpu_custom_call" | custom-call | flops 100000000 | bytes 3057664 | tf_op jit(solution)/shard_map/pallas_call | solution.py:37
  11.0 1.9 %collective-permute-start.3 = (bf16[3,14,32,256]{3,2,1,0:T(8,128)(2,1)S(1)}, bf16[3,14,32,256]{3,2,1,0:T(8,128)(2,1)S(1)}, u32[]{:S(2)}, u32[]{:S(2)}) collective-permute-start(bf16[3,14,32,256]{3,2,1,0:T(8,128)(2,1)S(1)} %get-tuple-element.45), channel_id=1, source_target_pairs={{0,4},{4,0},{8,12},{12,8},{16,20},{20,16},{24,28},{28,24},{1,5},{5... | collective-permute-start | bytes 2064392 | tf_op jit(solution)/shard_map/ppermute | solution.py:32
  12.9 3.0 %collective-permute-start.4 = (bf16[3,8,32,256]{3,2,1,0:T(8,128)(2,1)S(1)}, bf16[3,8,32,256]{3,2,1,0:T(8,128)(2,1)S(1)}, u32[]{:S(2)}, u32[]{:S(2)}) collective-permute-start(bf16[3,8,32,256]{3,2,1,0:T(8,128)(2,1)S(1)} %get-tuple-element.54), channel_id=1, source_target_pairs={{4,8},{8,4},{12,16},{16,12},{20,24},{24,20},{5,9},{9,5},{13,17},{1... | collective-permute-start | bytes 1179656 | tf_op jit(solution)/shard_map/ppermute | solution.py:32
  15.9 3.4 %collective-permute-start.2 = (bf16[15,32,256]{2,1,0:T(8,128)(2,1)S(1)}, bf16[15,32,256]{2,1,0:T(8,128)(2,1)S(1)}, u32[]{:S(2)}, u32[]{:S(2)}) collective-permute-start(bf16[15,32,256]{2,1,0:T(8,128)(2,1)S(1)} %get-tuple-element.44), channel_id=1, source_target_pairs={{4,8},{8,4},{12,16},{16,12},{20,24},{24,20},{5,9},{9,5},{13,17},{1... | collective-permute-start | bytes 737288 | tf_op jit(solution)/shard_map/ppermute | solution.py:32
  19.4 0.0 collective-permute-done.3.near
  19.4 4.4 %shard_map.103 = (f32[3,5,16,256]{3,2,1,0:T(8,128)S(1)}, bf16[3,2,14,32,256]{4,3,2,1,0:T(8,128)(2,1)S(1)}) custom-call(bf16[4,8,32,256]{3,2,1,0:T(8,128)(2,1)S(1)} %get-tuple-element.33.own, bf16[3,14,32,256]{3,2,1,0:T(8,128)(2,1)S(1)} %collective-permute-done.3.near, bf16[4,3,32,256]{3,2,1,0:T(8,128)(2,1)S(1)} %collective-permute-done.yeven, ...), custom_call_target="tpu_custom_call" | custom-call | flops 6000000000 | bytes 5328896 | tf_op jit(solution)/shard_map/pallas_call | solution.py:37
  23.8 3.3 %collective-permute-done.4.far = bf16[3,8,32,256]{3,2,1,0:T(8,128)(2,1)S(1)} collective-permute-done((bf16[3,8,32,256]{3,2,1,0:T(8,128)(2,1)S(1)}, bf16[3,8,32,256]{3,2,1,0:T(8,128)(2,1)S(1)}, u32[]{:S(2)}, u32[]{:S(2)}) %collective-permute-start.4) | collective-permute-done | bytes 393248 | tf_op jit(solution)/shard_map/ppermute | solution.py:32
  27.1 1.4 %shard_map.104 = (f32[3,3,16,256]{3,2,1,0:T(8,128)S(1)}, bf16[3,3,8,32,256]{4,3,2,1,0:T(8,128)(2,1)S(1)}) custom-call(bf16[3,8,32,256]{3,2,1,0:T(8,128)(2,1)S(1)} %collective-permute-done.4.far, bf16[3,2,14,32,256]{4,3,2,1,0:T(8,128)(2,1)S(1)} %get-tuple-element.53.tail, bf16[192,768]{1,0:T(8,128)(2,1)S(1)} %get-tuple-element.46.wxy, ...), custom_call_target="tpu_custom_call" | custom-call | flops 3000000000 | bytes 5062656 | tf_op jit(solution)/shard_map/pallas_call | solution.py:37
  28.5 3.3 %collective-permute-done.2.corner = bf16[15,32,256]{2,1,0:T(8,128)(2,1)S(1)} collective-permute-done((bf16[15,32,256]{2,1,0:T(8,128)(2,1)S(1)}, bf16[15,32,256]{2,1,0:T(8,128)(2,1)S(1)}, u32[]{:S(2)}, u32[]{:S(2)}) %collective-permute-start.2) | collective-permute-done | bytes 245792 | tf_op jit(solution)/shard_map/ppermute | solution.py:32
  31.8 1.6 %shard_map.105 = f32[3,4,8,256]{3,2,1,0:T(8,128)} custom-call(bf16[15,32,256]{2,1,0:T(8,128)(2,1)S(1)} %collective-permute-done.2.corner, bf16[3,2,14,32,256]{4,3,2,1,0:T(8,128)(2,1)S(1)} %get-tuple-element.53.tail, bf16[3,3,8,32,256]{4,3,2,1,0:T(8,128)(2,1)S(1)} %get-tuple-element.56.face, f32[3,5,16,256]{3,2,1,0:T(8,128)S(1)} %get-tuple-element.57.mean, ...), custom_call_target="tpu_custom_call" | custom-call | flops 2000000000 | bytes 4673536 | tf_op jit(solution)/shard_map/pallas_call | solution.py:37
Async XLA Ops:
  0.0 1.0 %copy-start = (bf16[32,4,8,256]{3,2,1,0:T(8,128)(2,1)S(1)}, bf16[32,4,8,256]{3,2,1,0:T(8,128)(2,1)}, u32[]{:S(2)}) copy-start(bf16[32,4,8,256]{3,2,1,0:T(8,128)(2,1)} %feat_ref.1) | copy-start | bytes 1572868
  1.5 6.6 %collective-permute-start = (bf16[4,3,32,256]{3,2,1,0:T(8,128)(2,1)S(1)}, bf16[4,3,32,256]{3,2,1,0:T(8,128)(2,1)S(1)}, u32[]{:S(2)}, u32[]{:S(2)}) collective-permute-start(bf16[4,3,32,256]{3,2,1,0:T(8,128)(2,1)S(1)} %get-tuple-element.34), channel_id=1, source_target_pairs={{0,1},{1,0},{2,3},{3,2},{4,5},{5,4},{6,7},{7,6},{8,9},{9,8},{10,11... | collective-permute-start | bytes 589832 | tf_op jit(solution)/shard_map/ppermute | solution.py:32
  2.8 7.4 %collective-permute-start.1 = (bf16[4,3,32,256]{3,2,1,0:T(8,128)(2,1)S(1)}, bf16[4,3,32,256]{3,2,1,0:T(8,128)(2,1)S(1)}, u32[]{:S(2)}, u32[]{:S(2)}) collective-permute-start(bf16[4,3,32,256]{3,2,1,0:T(8,128)(2,1)S(1)} %get-tuple-element.35), channel_id=1, source_target_pairs={{1,2},{2,1},{5,6},{6,5},{9,10},{10,9},{13,14},{14,13},{17,18},{18,... | collective-permute-start | bytes 589832 | tf_op jit(solution)/shard_map/ppermute | solution.py:32
  11.0 8.3 %collective-permute-start.3 = (bf16[3,14,32,256]{3,2,1,0:T(8,128)(2,1)S(1)}, bf16[3,14,32,256]{3,2,1,0:T(8,128)(2,1)S(1)}, u32[]{:S(2)}, u32[]{:S(2)}) collective-permute-start(bf16[3,14,32,256]{3,2,1,0:T(8,128)(2,1)S(1)} %get-tuple-element.45), channel_id=1, source_target_pairs={{0,4},{4,0},{8,12},{12,8},{16,20},{20,16},{24,28},{28,24},{1,5},{5... | collective-permute-start | bytes 2064392 | tf_op jit(solution)/shard_map/ppermute | solution.py:32
  12.9 14.2 %collective-permute-start.4 = (bf16[3,8,32,256]{3,2,1,0:T(8,128)(2,1)S(1)}, bf16[3,8,32,256]{3,2,1,0:T(8,128)(2,1)S(1)}, u32[]{:S(2)}, u32[]{:S(2)}) collective-permute-start(bf16[3,8,32,256]{3,2,1,0:T(8,128)(2,1)S(1)} %get-tuple-element.54), channel_id=1, source_target_pairs={{4,8},{8,4},{12,16},{16,12},{20,24},{24,20},{5,9},{9,5},{13,17},{1... | collective-permute-start | bytes 1179656 | tf_op jit(solution)/shard_map/ppermute | solution.py:32
  15.9 15.8 %collective-permute-start.2 = (bf16[15,32,256]{2,1,0:T(8,128)(2,1)S(1)}, bf16[15,32,256]{2,1,0:T(8,128)(2,1)S(1)}, u32[]{:S(2)}, u32[]{:S(2)}) collective-permute-start(bf16[15,32,256]{2,1,0:T(8,128)(2,1)S(1)} %get-tuple-element.44), channel_id=1, source_target_pairs={{4,8},{8,4},{12,16},{16,12},{20,24},{24,20},{5,9},{9,5},{13,17},{1... | collective-permute-start | bytes 737288 | tf_op jit(solution)/shard_map/ppermute | solution.py:32

commit v3 on v2

--- a/solution.py
+++ b/solution.py
@@ -55,11 +55,20 @@
     return ((row // channels == col % rows) & (row % channels == col // rows)).astype(F32).astype(BF16)
 
 
-def pack_kernel(feat_ref, own_ref, even_ref, odd_ref, far_ref):
+def pack_kernel(feat_hbm, *refs):
+    count = (len(refs) - 6) // 2
+    own_ref, even_ref, odd_ref, far_ref = refs[count : count + 4]
+    feat_ref, sem = refs[-2:]
+    copies = [pltpu.make_async_copy(feat_hbm, feat_ref, sem.at[count])]
+    for n in range(count):
+        copies.append(pltpu.make_async_copy(refs[n], refs[count + 4 + n], sem.at[n]))
+    for copy in copies:
+        copy.start()
     channels, depth, rows, cols = feat_ref.shape
     size = channels * rows
     order = cell_order(channels, rows)
     part_z, part_y = odd("gz"), odd("gy")
+    copies[0].wait()
     for z in range(depth):
         value = feat_ref[:, z].astype(F32).reshape(size, cols).astype(BF16)
         value = matmul(order, value).astype(BF16).reshape(rows, channels, cols)
@@ -69,30 +78,19 @@
         for row in range(HALO):
             even_ref[z, row] = own_ref[z, first_even + row]
             odd_ref[z, row] = own_ref[z, first_odd + row]
-    for layer in range(HALO):
+    for layer in range(2):
         far_ref[layer] = own_ref[depth - 1 - layer]
+    for copy in copies[1:]:
+        copy.wait()
 
 
 def weights_kernel(
-    scale1_hbm, shift1_hbm, conv1_hbm, bias1_hbm, scale2_hbm, shift2_hbm, conv2_hbm, bias2_hbm, flow_hbm,
-    wxy_ref, wyz_ref, wza_ref, wzb_ref, wxe_ref, wye_ref,
-    vxy_ref, vyz_ref, vza_ref, vzb_ref, vxe_ref, vye_ref, vf_ref,
+    scale1, shift1, conv1, bias1, scale2, shift2, conv2, bias2, flow,
+    wxy_ref, wyz_ref, wza_ref, wzb_ref, wxe_ref, wye_ref, wzc_ref,
+    vxy_ref, vyz_ref, vza_ref, vzb_ref, vxe_ref, vye_ref, vzc_ref, vf_ref,
     s1_ref, t1_ref, s2_ref, t2_ref, const_ref,
-    scale1, shift1, conv1, bias1, scale2, shift2, conv2, bias2, flow, taps, folds, sem,
+    taps, folds,
 ):
-    copies = [
-        pltpu.make_async_copy(source, target, sem.at[n])
-        for n, (source, target) in enumerate(
-            (
-                (scale1_hbm, scale1), (shift1_hbm, shift1), (conv1_hbm, conv1), (bias1_hbm, bias1),
-                (scale2_hbm, scale2), (shift2_hbm, shift2), (conv2_hbm, conv2), (bias2_hbm, bias2), (flow_hbm, flow),
-            )
-        )
-    ]
-    for copy in copies:
-        copy.start()
-    for copy in copies:
-        copy.wait()
     c = conv1.shape[-1]
     part_z = odd("gz")
 
@@ -145,8 +143,9 @@
     banded(wzb_ref, lambda g, i: taps[along_z(i), g])
     banded(wxe_ref, lambda g, i: taps[i, g])
     banded(wye_ref, lambda g, i: taps[along_z(g), i])
-
-    def banded_flow(ref, pick, place):
+    banded(wzc_ref, lambda g, i: taps[along_z(i), g])
+
+    def banded_flow(ref, pick, place, steps=3):
         cols = ref.shape[1]
         height = ref.shape[0] // 12
         band = place(iota((height, cols), 1) // c) - iota((height, cols), 0)
@@ -154,7 +153,7 @@
             for g in range(3):
                 for k in range(2):
                     block = jnp.zeros((height, cols), F32)
-                    for i in range(3):
+                    for i in range(steps):
                         row, col = pick(g, i)
                         block = jnp.where(band == i, folds[row, col, part, k : k + 1, :cols], block)
                     at = ((part * 3 + g) * 2 + k) * height
@@ -168,6 +167,7 @@
     banded_flow(vzb_ref, lambda g, i: (along_z(i), g), lambda b: b + past)
     banded_flow(vxe_ref, lambda g, i: (i, g), lambda b: jnp.where(b < EDGE, b, b + middle))
     banded_flow(vye_ref, lambda g, i: (along_z(g), i), lambda b: jnp.where(b < EDGE, b, b + middle))
+    banded_flow(vzc_ref, lambda g, i: (along_z(i), g), lambda b: b, 1)
     cols = vf_ref.shape[1]
     plain = matmul(flow[...], short)
     for k in range(2):
@@ -280,9 +280,9 @@
 
 
 def rim_kernel(
-    own, yeven, yodd, wye, wzb, vye, vza, s1, t1, s2, t2, near_ref, corner_ref, unit, part,
+    own, yeven, yodd, wyz, wzc, vyz, vzc, s1, t1, s2, t2, near_ref, corner_ref, unit,
 ):
-    depth, rows, c, cols = own.shape
+    depth, rows, c, _ = own.shape
     for layer in range(HALO):
         near_ref[layer, :rows] = own[layer]
         near_ref[layer, rows : rows + HALO] = yeven[layer]
@@ -301,32 +301,22 @@
 
     for z in range(3):
         layer = depth - 3 + z
-        place(own[layer, :2], z, HALO, None)
-        place(own[layer, rows - 2 :], z, HALO + rows - 2, None)
+        place(own[layer], z, HALO, None)
         place(yeven[layer], z, at_even, valid_even)
         place(yodd[layer], z, at_odd, valid_odd)
-    keeps = (edge_scale(s2, EDGE, 2, low_y), edge_scale(s2, EDGE, -2, high_y))
-    cells = []
-    for keep, window in zip(keeps, (range(EDGE + 2), range(rows + 1, rows + 6))):
-        data = stack([unit[1, i, y] for i in range(3) for y in window])
-        cells.append(activate(matmul(wye[...], data), s2[: EDGE * c] * keep, t2[: EDGE * c] * keep, c))
-    none = jnp.zeros((2 * c, cols), BF16)
-    ends = []
-    for at in (0, rows + 1):
-        data = stack([p for j in range(3) for p in (none, *(unit[j, z, at + 2] for z in range(3)))])
-        ends.append(activate(matmul(wzb[...], data)[2 * c :], s2[:c], t2[:c], c))
-    flow = yz_parts(vye, stack(cells))[0]
-    ends = [along_x(matmul(vza[...], stack([none, none, cell]))) for cell in ends]
-    height = part.shape[1]
-    part[0] = 0.5 * flow[:height]
-    part[1] = 0.5 * flow[height:]
-    part[2] = jnp.zeros((height, cols), F32)
-    for at, flow in zip((0, rows + 1), ends):
-        step = flow.shape[0] // 2
-        part[0, at : at + 1] = part[0, at : at + 1] + 0.5 * flow[depth : depth + 1]
-        part[2, at : at + 1] = 0.5 * flow[step + depth : step + depth + 1]
-    for k in range(3):
-        value = part[k]
+    keeps = (edge_scale(s2, SPAN, 2, low_y), edge_scale(s2, SPAN, -2, high_y))
+    act_yz = []
+    for w, keep in enumerate(keeps):
+        data = stack([unit[1, i, w * SPAN : w * SPAN + WIDE] for i in range(3)])
+        act_yz.append(activate(matmul(wyz[...], data), s2[...] * keep, t2[...] * keep, c))
+    act_xz = []
+    for y in range(rows + 2):
+        data = stack([unit[j, z, y + 2] for j in range(3) for z in range(3)])
+        act_xz.append(activate(matmul(wzc[...], data), s2[:c], t2[:c], c))
+    flow_yz = 0.5 * yz_parts(vyz, stack(act_yz))[0]
+    flow_xz = 0.5 * along_x(matmul(vzc[...], stack(act_xz)))
+    height = flow_xz.shape[0] // 2
+    for k, value in enumerate((flow_yz[:height] + flow_xz[:height], flow_yz[height:], flow_xz[height:])):
         top = value.astype(BF16)
         corner_ref[4 * HALO + k, :height] = top
         corner_ref[4 * HALO + k, height:] = (value - top.astype(F32)).astype(BF16)
@@ -402,15 +392,16 @@
 ):
     _, rows, c, cols = far.shape
     _, valid_far, _, _ = valid_sides()
-    for z in range(HALO):
+    for z in range(2):
         for j, moved in enumerate(normalized(far[z], s1, t1, valid_far)):
             face[j, z] = moved
 
     def read(j, z, y):
         return tail[j, z, y + HALO] if z < 2 else face[j, z - 2, y]
 
-    keep = edge_scale(s2, EDGE, -2, valid_far)
-    scale, shift = s2[: EDGE * c] * keep, t2[: EDGE * c] * keep
+    keep = edge_scale(s2, 2, -1, valid_far)
+    scale, shift = s2[: 2 * c] * keep, t2[: 2 * c] * keep
+    none = jnp.zeros((c, cols), BF16)
     gap = jnp.zeros((EDGE * c, cols), BF16)
 
     def middle(cells):
@@ -420,16 +411,16 @@
     data = stack([face[j, 0] for j in range(3)])
     act_xy = activate(matmul(wxy[...], data), s2[...], t2[...], c)
     act_yz = []
-    for z in range(1, 4):
+    for z in range(1, 3):
         data = stack([tail[1, i, inner] if i < 2 else face[1, i - 2] for i in range(z - 1, z + 2)])
         act_yz.append(activate(matmul(wyz[...], data), s2[...], t2[...], c, valid_far if z > 1 else None))
     act_xz = []
     for y in range(rows):
-        data = stack([read(j, z, y) for j in range(3) for z in range(EDGE + 2)])
-        act_xz.append(activate(matmul(wzb[...], data), scale, shift, c))
+        data = stack([p for j in range(3) for p in (*(read(j, z, y) for z in range(4)), none)])
+        act_xz.append(activate(matmul(wzb[...], data)[: 2 * c], scale, shift, c))
     flow_xy = {2: along_x(matmul(vxy[...], middle(act_xy)))}
-    flow_yz = {z: yz_parts(vyz, middle(act_yz[z - 1])) for z in range(1, 4)}
-    flow_xz = [along_x(matmul(vzb[...], cells.reshape(-1, cols))) for cells in act_xz]
+    flow_yz = {z: yz_parts(vyz, middle(act_yz[z - 1])) for z in range(1, 3)}
+    flow_xz = [along_x(matmul(vzb[...], stack([cells, none]))) for cells in act_xz]
     fxz[...] = jnp.zeros_like(fxz)
     for y, flow in enumerate(flow_xz):
         half = flow.shape[0] // 2
@@ -543,35 +534,41 @@
     shape = jax.ShapeDtypeStruct
     cells = functools.partial(shape, dtype=BF16)
     side = cells((depth, HALO, c, cols))
-    own, send_even, send_odd, send_far = call(
-        pack_kernel,
-        [cells((depth, rows, c, cols)), side, side, cells((HALO, rows, c, cols))],
-        [features], 2 * features.size * c * rows, 6,
-    )
-    yeven = swap(send_even, "gy", 0)
-    yodd = swap(send_odd, "gy", 1)
-    far = swap(send_far, "gz", 1)
-
-    broad = rows + 2 * HALO
-    high = -(-(rows + 2) // 8) * 8
-    deep = -(-(depth + 2) // 8) * 8
     params = [
         scale_first[None], shift_first[None], conv_first, bias_first[None],
         scale_second[None], shift_second[None], conv_second, bias_second[None], flow_weight,
     ]
     params = [pltpu.with_memory_space_constraint(p, pltpu.HBM) for p in params]
-    wxy, wyz, wza, wzb, wxe, wye, vxy, vyz, vza, vzb, vxe, vye, vf, *rest = call(
+    own, send_even, send_odd, send_far, *params = call(
+        pack_kernel,
+        [cells((depth, rows, c, cols)), side, side, cells((2, rows, c, cols))]
+        + [shape(p.shape, p.dtype) for p in params],
+        [pltpu.with_memory_space_constraint(features, pltpu.HBM), *params],
+        2 * features.size * c * rows, 6,
+        [pltpu.VMEM(features.shape, BF16), pltpu.SemaphoreType.DMA((len(params) + 1,))],
+        HBM,
+    )
+    yeven = swap(send_even, "gy", 0)
+    yodd = swap(send_odd, "gy", 1)
+    far = swap(send_far, "gz", 1)
+
+    broad = rows + 2 * HALO
+    high = -(-(rows + 2) // 8) * 8
+    deep = -(-(depth + 2) // 8) * 8
+    wxy, wyz, wza, wzb, wxe, wye, wzc, vxy, vyz, vza, vzb, vxe, vye, vzc, vf, *rest = call(
         weights_kernel,
         [
             cells((SPAN * c, 3 * WIDE * c)),
             cells((SPAN * c, 3 * WIDE * c)),
             cells(((depth + 1) * c, 3 * (depth + 3) * c)),
             *[cells((EDGE * c, 3 * (EDGE + 2) * c))] * 3,
+            cells((c, 9 * c)),
             cells((12 * high, (rows + 4) * c)),
             cells((12 * high, (rows + 4) * c)),
             cells((12 * deep, (depth + 1) * c)),
             cells((12 * deep, EDGE * c)),
             *[cells((12 * high, 2 * EDGE * c))] * 2,
+            cells((12 * high, (rows + 2) * c)),
             cells((2 * high, (rows + 2) * c)),
             shape((rows * c, cols), F32),
             shape((rows * c, cols), F32),
@@ -582,20 +579,17 @@
         params,
         2 * 10**9, 10,
         [
-            *(pltpu.VMEM(p.shape, p.dtype) for p in params),
             pltpu.VMEM((3, 3, c, 3 * WIDE * c), F32),
             pltpu.VMEM((3, 3, 2, 2, (rows + 4) * c), F32),
-            pltpu.SemaphoreType.DMA((len(params),)),
         ],
-        HBM,
     )
     assert c == 2 * high
     send_near, send_corner = call(
         rim_kernel,
         [cells((HALO, broad, c, cols)), cells((4 * HALO + 3, c, cols))],
-        [own, yeven, yodd, wye, wzb, vye, vza, *rest[:4]],
+        [own, yeven, yodd, wyz, wzc, vyz, vzc, *rest[:4]],
         10**8, 10,
-        [pltpu.VMEM((3, 3, broad, c, cols), BF16), pltpu.VMEM((3, high, cols), F32)],
+        [pltpu.VMEM((3, 3, broad, c, cols), BF16)],
     )
     corner = swap(send_corner, "gz", 1)
     near = swap(send_near, "gz", 0)
@@ -618,7 +612,7 @@
     )
     more, face = call(
         functools.partial(mid_kernel, depth + 1),
-        [shape((3, 3, high, cols), F32), cells((3, HALO, rows, c, cols))],
+        [shape((3, 3, high, cols), F32), cells((3, 2, rows, c, cols))],
         [far, tail, wxy, wyz, wzb, vxy, vyz, vzb, vf, *rest],
         3 * 10**9, 12,
         [pltpu.VMEM((2, deep, high, cols), F32)],

time: 33.6 us -> 31.2 us (0.929)
  waiting for transfers between devices: 8.72 us -> 7.3 us
  local copies, waits for them, and re-layouts: 1.04 us -> 0 us
    ppermute x5, waiting for transfers between devices: 8.72 us -> 7.3 us  [swap(): return lax.ppermute(value, axis, pairs)]
    unnamed x2 -> x0, local copies, waits for them, and re-layouts: 1.04 us -> none
  transfers between devices with their start and end apart: 5 -> 5, of which waited for: 3 -> 4; matrix products, arithmetic and copies ran while one was open for 0% -> 0% of each run, Pallas kernels for 27% -> 25%
where the time goes in v3:
time: 31.2 us; the launch traced here: 31.1 us
  Pallas kernels  12.1 us (39%)
  starting transfers between devices  11.6 us (37%)
  waiting for transfers between devices  7.3 us (23%)
    pallas_call x6, Pallas kernels, call(): pl.pallas_call(kernel, out_shape=outs, in_specs=[space] * len(args), out_...  12.1 us
    ppermute x5, starting transfers between devices, swap(): return lax.ppermute(value, axis, pairs)  11.6 us
    ppermute x5, waiting for transfers between devices, swap(): return lax.ppermute(value, axis, pairs)  7.3 us
  transfers between devices with their start and end apart: 5, of which 4 were waited for; matrix products, arithmetic and copies ran while one was open for 0% of the time, Pallas kernels for 25%

profile of v3, /device:TPU:19, one launch (start us, length us, event | category | flops | bytes accessed | tf_op | source)
XLA Modules:
  0.0 31.1 jit_solution(3185703512982771080)
XLA Ops:
  0.0 1.5 %shard_map.100 = (bf16[4,8,32,256]{3,2,1,0:T(8,128)(2,1)S(1)}, bf16[4,3,32,256]{3,2,1,0:T(8,128)(2,1)S(1)}, bf16[4,3,32,256]{3,2,1,0:T(8,128)(2,1)S(1)}, bf16[2,...) custom-call(bf16[32,4,8,256]{3,2,1,0:T(8,128)(2,1)} %feat_hbm.1, ...), custom_call_target="tpu_custom_call" | custom-call | flops 134217728 | bytes 1779456 | tf_op jit(solution)/shard_map/pallas_call | solution.py:37
  1.6 1.4 %collective-permute-start = (bf16[4,3,32,256]{3,2,1,0:T(8,128)(2,1)S(1)}, bf16[4,3,32,256]{3,2,1,0:T(8,128)(2,1)S(1)}, u32[]{:S(2)}, u32[]{:S(2)}) collective-permute-start(bf16[4,3,32,256]{3,2,1,0:T(8,128)(2,1)S(1)} %get-tuple-element.45), channel_id=1, source_target_pairs={{0,1},{1,0},{2,3},{3,2},{4,5},{5,4},{6,7},{7,6},{8,9},{9,8},{10,11... | collective-permute-start | bytes 589832 | tf_op jit(solution)/shard_map/ppermute | solution.py:32
  2.9 1.9 %collective-permute-start.1 = (bf16[4,3,32,256]{3,2,1,0:T(8,128)(2,1)S(1)}, bf16[4,3,32,256]{3,2,1,0:T(8,128)(2,1)S(1)}, u32[]{:S(2)}, u32[]{:S(2)}) collective-permute-start(bf16[4,3,32,256]{3,2,1,0:T(8,128)(2,1)S(1)} %get-tuple-element.46), channel_id=1, source_target_pairs={{1,2},{2,1},{5,6},{6,5},{9,10},{10,9},{13,14},{14,13},{17,18},{18,... | collective-permute-start | bytes 589832 | tf_op jit(solution)/shard_map/ppermute | solution.py:32
  4.8 2.3 %shard_map.101 = (bf16[192,768]{1,0:T(8,128)(2,1)S(1)}, bf16[192,768]{1,0:T(8,128)(2,1)S(1)}, bf16[160,672]{1,0:T(8,128)(2,1)S(1)}, bf16[96,480]{1,0:T(8,128)(2,...) custom-call(f32[1,32]{1,0:T(1,128)S(1)} %get-tuple-element.47.scale1, ...), custom_call_target="tpu_custom_call" | custom-call | flops 2000000000 | bytes 2722688 | tf_op jit(solution)/shard_map/pallas_call | solution.py:37
  7.1 0.3 collective-permute-done.yeven
  7.4 2.9 %collective-permute-done.1.yodd = bf16[4,3,32,256]{3,2,1,0:T(8,128)(2,1)S(1)} collective-permute-done((bf16[4,3,32,256]{3,2,1,0:T(8,128)(2,1)S(1)}, bf16[4,3,32,256]{3,2,1,0:T(8,128)(2,1)S(1)}, u32[]{:S(2)}, u32[]{:S(2)}) %collective-permute-start.1) | collective-permute-done | bytes 196640 | tf_op jit(solution)/shard_map/ppermute | solution.py:32
  10.3 1.2 %shard_map.102 = (bf16[3,14,32,256]{3,2,1,0:T(8,128)(2,1)S(1)}, bf16[15,32,256]{2,1,0:T(8,128)(2,1)S(1)}) custom-call(bf16[4,8,32,256]{3,2,1,0:T(8,128)(2,1)S(1)} %get-tuple-element.44.own, bf16[4,3,32,256]{3,2,1,0:T(8,128)(2,1)S(1)} %collective-permute-done.yeven, bf16[4,3,32,256]{3,2,1,0:T(8,128)(2,1)S(1)} %collective-permute-done.1.yodd, ...), custom_call_target="tpu_custom_call" | custom-call | flops 100000000 | bytes 3352576 | tf_op jit(solution)/shard_map/pallas_call | solution.py:37
  11.5 1.9 %collective-permute-start.3 = (bf16[3,14,32,256]{3,2,1,0:T(8,128)(2,1)S(1)}, bf16[3,14,32,256]{3,2,1,0:T(8,128)(2,1)S(1)}, u32[]{:S(2)}, u32[]{:S(2)}) collective-permute-start(bf16[3,14,32,256]{3,2,1,0:T(8,128)(2,1)S(1)} %get-tuple-element.65), channel_id=1, source_target_pairs={{0,4},{4,0},{8,12},{12,8},{16,20},{20,16},{24,28},{28,24},{1,5},{5... | collective-permute-start | bytes 2064392 | tf_op jit(solution)/shard_map/ppermute | solution.py:32
  13.4 3.0 %collective-permute-start.4 = (bf16[2,8,32,256]{3,2,1,0:T(8,128)(2,1)S(1)}, bf16[2,8,32,256]{3,2,1,0:T(8,128)(2,1)S(1)}, u32[]{:S(2)}, u32[]{:S(2)}) collective-permute-start(bf16[2,8,32,256]{3,2,1,0:T(8,128)(2,1)S(1)} %get-tuple-element.73), channel_id=1, source_target_pairs={{4,8},{8,4},{12,16},{16,12},{20,24},{24,20},{5,9},{9,5},{13,17},{1... | collective-permute-start | bytes 786440 | tf_op jit(solution)/shard_map/ppermute | solution.py:32
  16.4 3.4 %collective-permute-start.2 = (bf16[15,32,256]{2,1,0:T(8,128)(2,1)S(1)}, bf16[15,32,256]{2,1,0:T(8,128)(2,1)S(1)}, u32[]{:S(2)}, u32[]{:S(2)}) collective-permute-start(bf16[15,32,256]{2,1,0:T(8,128)(2,1)S(1)} %get-tuple-element.64), channel_id=1, source_target_pairs={{4,8},{8,4},{12,16},{16,12},{20,24},{24,20},{5,9},{9,5},{13,17},{1... | collective-permute-start | bytes 737288 | tf_op jit(solution)/shard_map/ppermute | solution.py:32
  19.9 0.0 collective-permute-done.3.near
  19.9 4.3 %shard_map.103 = (f32[3,5,16,256]{3,2,1,0:T(8,128)S(1)}, bf16[3,2,14,32,256]{4,3,2,1,0:T(8,128)(2,1)S(1)}) custom-call(bf16[4,8,32,256]{3,2,1,0:T(8,128)(2,1)S(1)} %get-tuple-element.44.own, bf16[3,14,32,256]{3,2,1,0:T(8,128)(2,1)S(1)} %collective-permute-done.3.near, bf16[4,3,32,256]{3,2,1,0:T(8,128)(2,1)S(1)} %collective-permute-done.yeven, ...), custom_call_target="tpu_custom_call" | custom-call | flops 6000000000 | bytes 5328896 | tf_op jit(solution)/shard_map/pallas_call | solution.py:37
  24.2 0.6 %collective-permute-done.4.far = bf16[2,8,32,256]{3,2,1,0:T(8,128)(2,1)S(1)} collective-permute-done((bf16[2,8,32,256]{3,2,1,0:T(8,128)(2,1)S(1)}, bf16[2,8,32,256]{3,2,1,0:T(8,128)(2,1)S(1)}, u32[]{:S(2)}, u32[]{:S(2)}) %collective-permute-start.4) | collective-permute-done | bytes 262176 | tf_op jit(solution)/shard_map/ppermute | solution.py:32
  24.8 1.2 %shard_map.104 = (f32[3,3,16,256]{3,2,1,0:T(8,128)S(1)}, bf16[3,2,8,32,256]{4,3,2,1,0:T(8,128)(2,1)S(1)}) custom-call(bf16[2,8,32,256]{3,2,1,0:T(8,128)(2,1)S(1)} %collective-permute-done.4.far, bf16[3,2,14,32,256]{4,3,2,1,0:T(8,128)(2,1)S(1)} %get-tuple-element.72.tail, bf16[192,768]{1,0:T(8,128)(2,1)S(1)} %get-tuple-element.66.wxy, ...), custom_call_target="tpu_custom_call" | custom-call | flops 3000000000 | bytes 4538368 | tf_op jit(solution)/shard_map/pallas_call | solution.py:37
  25.9 3.5 %collective-permute-done.2.corner = bf16[15,32,256]{2,1,0:T(8,128)(2,1)S(1)} collective-permute-done((bf16[15,32,256]{2,1,0:T(8,128)(2,1)S(1)}, bf16[15,32,256]{2,1,0:T(8,128)(2,1)S(1)}, u32[]{:S(2)}, u32[]{:S(2)}) %collective-permute-start.2) | collective-permute-done | bytes 245792 | tf_op jit(solution)/shard_map/ppermute | solution.py:32
  29.4 1.6 %shard_map.105 = f32[3,4,8,256]{3,2,1,0:T(8,128)} custom-call(bf16[15,32,256]{2,1,0:T(8,128)(2,1)S(1)} %collective-permute-done.2.corner, bf16[3,2,14,32,256]{4,3,2,1,0:T(8,128)(2,1)S(1)} %get-tuple-element.72.tail, bf16[3,2,8,32,256]{4,3,2,1,0:T(8,128)(2,1)S(1)} %get-tuple-element.76.face, f32[3,5,16,256]{3,2,1,0:T(8,128)S(1)} %get-tuple-element.77.mean, ...), custom_call_target="tpu_custom_call" | custom-call | flops 2000000000 | bytes 4280320 | tf_op jit(solution)/shard_map/pallas_call | solution.py:37
Async XLA Ops:
  1.6 5.9 %collective-permute-start = (bf16[4,3,32,256]{3,2,1,0:T(8,128)(2,1)S(1)}, bf16[4,3,32,256]{3,2,1,0:T(8,128)(2,1)S(1)}, u32[]{:S(2)}, u32[]{:S(2)}) collective-permute-start(bf16[4,3,32,256]{3,2,1,0:T(8,128)(2,1)S(1)} %get-tuple-element.45), channel_id=1, source_target_pairs={{0,1},{1,0},{2,3},{3,2},{4,5},{5,4},{6,7},{7,6},{8,9},{9,8},{10,11... | collective-permute-start | bytes 589832 | tf_op jit(solution)/shard_map/ppermute | solution.py:32
  2.9 7.4 %collective-permute-start.1 = (bf16[4,3,32,256]{3,2,1,0:T(8,128)(2,1)S(1)}, bf16[4,3,32,256]{3,2,1,0:T(8,128)(2,1)S(1)}, u32[]{:S(2)}, u32[]{:S(2)}) collective-permute-start(bf16[4,3,32,256]{3,2,1,0:T(8,128)(2,1)S(1)} %get-tuple-element.46), channel_id=1, source_target_pairs={{1,2},{2,1},{5,6},{6,5},{9,10},{10,9},{13,14},{14,13},{17,18},{18,... | collective-permute-start | bytes 589832 | tf_op jit(solution)/shard_map/ppermute | solution.py:32
  11.5 8.3 %collective-permute-start.3 = (bf16[3,14,32,256]{3,2,1,0:T(8,128)(2,1)S(1)}, bf16[3,14,32,256]{3,2,1,0:T(8,128)(2,1)S(1)}, u32[]{:S(2)}, u32[]{:S(2)}) collective-permute-start(bf16[3,14,32,256]{3,2,1,0:T(8,128)(2,1)S(1)} %get-tuple-element.65), channel_id=1, source_target_pairs={{0,4},{4,0},{8,12},{12,8},{16,20},{20,16},{24,28},{28,24},{1,5},{5... | collective-permute-start | bytes 2064392 | tf_op jit(solution)/shard_map/ppermute | solution.py:32
  13.4 11.4 %collective-permute-start.4 = (bf16[2,8,32,256]{3,2,1,0:T(8,128)(2,1)S(1)}, bf16[2,8,32,256]{3,2,1,0:T(8,128)(2,1)S(1)}, u32[]{:S(2)}, u32[]{:S(2)}) collective-permute-start(bf16[2,8,32,256]{3,2,1,0:T(8,128)(2,1)S(1)} %get-tuple-element.73), channel_id=1, source_target_pairs={{4,8},{8,4},{12,16},{16,12},{20,24},{24,20},{5,9},{9,5},{13,17},{1... | collective-permute-start | bytes 786440 | tf_op jit(solution)/shard_map/ppermute | solution.py:32
  16.4 13.0 %collective-permute-start.2 = (bf16[15,32,256]{2,1,0:T(8,128)(2,1)S(1)}, bf16[15,32,256]{2,1,0:T(8,128)(2,1)S(1)}, u32[]{:S(2)}, u32[]{:S(2)}) collective-permute-start(bf16[15,32,256]{2,1,0:T(8,128)(2,1)S(1)} %get-tuple-element.64), channel_id=1, source_target_pairs={{4,8},{8,4},{12,16},{16,12},{20,24},{24,20},{5,9},{9,5},{13,17},{1... | collective-permute-start | bytes 737288 | tf_op jit(solution)/shard_map/ppermute | solution.py:32

commit v4 on v3

--- a/solution.py
+++ b/solution.py
@@ -282,7 +282,7 @@
 def rim_kernel(
     own, yeven, yodd, wyz, wzc, vyz, vzc, s1, t1, s2, t2, near_ref, corner_ref, unit,
 ):
-    depth, rows, c, _ = own.shape
+    depth, rows, c, cols = own.shape
     for layer in range(HALO):
         near_ref[layer, :rows] = own[layer]
         near_ref[layer, rows : rows + HALO] = yeven[layer]
@@ -316,10 +316,10 @@
     flow_yz = 0.5 * yz_parts(vyz, stack(act_yz))[0]
     flow_xz = 0.5 * along_x(matmul(vzc[...], stack(act_xz)))
     height = flow_xz.shape[0] // 2
-    for k, value in enumerate((flow_yz[:height] + flow_xz[:height], flow_yz[height:], flow_xz[height:])):
-        top = value.astype(BF16)
-        corner_ref[4 * HALO + k, :height] = top
-        corner_ref[4 * HALO + k, height:] = (value - top.astype(F32)).astype(BF16)
+    corner_ref[4 * HALO, :height] = (flow_yz[:height] + flow_xz[:height]).astype(BF16)
+    corner_ref[4 * HALO, height:] = flow_yz[height:].astype(BF16)
+    corner_ref[4 * HALO + 1, :height] = flow_xz[height:].astype(BF16)
+    corner_ref[4 * HALO + 1, height:] = jnp.zeros((height, cols), BF16)
 
 
 def near_kernel(
@@ -515,7 +515,8 @@
                 if layer < start:
                     value = value + mean[k, at]
                 else:
-                    value = value + corner[4 * HALO + k, :height].astype(F32) + corner[4 * HALO + k, height:].astype(F32)
+                    half = slice(k % 2 * height, (k % 2 + 1) * height)
+                    value = value + corner[4 * HALO + k // 2, half].astype(F32)
                 total[k, at] = value * keep
     part_z = odd("gz")
     for k in range(3):
@@ -586,7 +587,7 @@
     assert c == 2 * high
     send_near, send_corner = call(
         rim_kernel,
-        [cells((HALO, broad, c, cols)), cells((4 * HALO + 3, c, cols))],
+        [cells((HALO, broad, c, cols)), cells((4 * HALO + 2, c, cols))],
         [own, yeven, yodd, wyz, wzc, vyz, vzc, *rest[:4]],
         10**8, 10,
         [pltpu.VMEM((3, 3, broad, c, cols), BF16)],

time: 31.2 us -> 30.9 us (level)
  waiting for transfers between devices: 7.3 us -> 6.95 us
    ppermute x5, waiting for transfers between devices: 7.3 us -> 6.95 us  [swap(): return lax.ppermute(value, axis, pairs)]
where the time goes in v4:
time: 30.9 us; the launch traced here: 30.7 us
  Pallas kernels  12.1 us (39%)
  starting transfers between devices  11.6 us (38%)
  waiting for transfers between devices  6.95 us (22%)
    pallas_call x6, Pallas kernels, call(): pl.pallas_call(kernel, out_shape=outs, in_specs=[space] * len(args), out_...  12.1 us
    ppermute x5, starting transfers between devices, swap(): return lax.ppermute(value, axis, pairs)  11.6 us
    ppermute x5, waiting for transfers between devices, swap(): return lax.ppermute(value, axis, pairs)  6.95 us
  transfers between devices with their start and end apart: 5, of which 4 were waited for; matrix products, arithmetic and copies ran while one was open for 0% of the time, Pallas kernels for 25%

profile of v4, /device:TPU:19, one launch (start us, length us, event | category | flops | bytes accessed | tf_op | source)
XLA Modules:
  0.0 30.7 jit_solution(7807154672384352041)
XLA Ops:
  0.0 1.5 %shard_map.100 = (bf16[4,8,32,256]{3,2,1,0:T(8,128)(2,1)S(1)}, bf16[4,3,32,256]{3,2,1,0:T(8,128)(2,1)S(1)}, bf16[4,3,32,256]{3,2,1,0:T(8,128)(2,1)S(1)}, bf16[2,...) custom-call(bf16[32,4,8,256]{3,2,1,0:T(8,128)(2,1)} %feat_hbm.1, ...), custom_call_target="tpu_custom_call" | custom-call | flops 134217728 | bytes 1779456 | tf_op jit(solution)/shard_map/pallas_call | solution.py:37
  1.6 1.4 %collective-permute-start = (bf16[4,3,32,256]{3,2,1,0:T(8,128)(2,1)S(1)}, bf16[4,3,32,256]{3,2,1,0:T(8,128)(2,1)S(1)}, u32[]{:S(2)}, u32[]{:S(2)}) collective-permute-start(bf16[4,3,32,256]{3,2,1,0:T(8,128)(2,1)S(1)} %get-tuple-element.45), channel_id=1, source_target_pairs={{0,1},{1,0},{2,3},{3,2},{4,5},{5,4},{6,7},{7,6},{8,9},{9,8},{10,11... | collective-permute-start | bytes 589832 | tf_op jit(solution)/shard_map/ppermute | solution.py:32
  2.9 1.9 %collective-permute-start.1 = (bf16[4,3,32,256]{3,2,1,0:T(8,128)(2,1)S(1)}, bf16[4,3,32,256]{3,2,1,0:T(8,128)(2,1)S(1)}, u32[]{:S(2)}, u32[]{:S(2)}) collective-permute-start(bf16[4,3,32,256]{3,2,1,0:T(8,128)(2,1)S(1)} %get-tuple-element.46), channel_id=1, source_target_pairs={{1,2},{2,1},{5,6},{6,5},{9,10},{10,9},{13,14},{14,13},{17,18},{18,... | collective-permute-start | bytes 589832 | tf_op jit(solution)/shard_map/ppermute | solution.py:32
  4.8 2.3 %shard_map.101 = (bf16[192,768]{1,0:T(8,128)(2,1)S(1)}, bf16[192,768]{1,0:T(8,128)(2,1)S(1)}, bf16[160,672]{1,0:T(8,128)(2,1)S(1)}, bf16[96,480]{1,0:T(8,128)(2,...) custom-call(f32[1,32]{1,0:T(1,128)S(1)} %get-tuple-element.47.scale1, ...), custom_call_target="tpu_custom_call" | custom-call | flops 2000000000 | bytes 2722688 | tf_op jit(solution)/shard_map/pallas_call | solution.py:37
  7.1 0.3 collective-permute-done.yeven
  7.4 2.9 %collective-permute-done.1.yodd = bf16[4,3,32,256]{3,2,1,0:T(8,128)(2,1)S(1)} collective-permute-done((bf16[4,3,32,256]{3,2,1,0:T(8,128)(2,1)S(1)}, bf16[4,3,32,256]{3,2,1,0:T(8,128)(2,1)S(1)}, u32[]{:S(2)}, u32[]{:S(2)}) %collective-permute-start.1) | collective-permute-done | bytes 196640 | tf_op jit(solution)/shard_map/ppermute | solution.py:32
  10.3 1.2 %shard_map.102 = (bf16[3,14,32,256]{3,2,1,0:T(8,128)(2,1)S(1)}, bf16[14,32,256]{2,1,0:T(8,128)(2,1)S(1)}) custom-call(bf16[4,8,32,256]{3,2,1,0:T(8,128)(2,1)S(1)} %get-tuple-element.44.own, bf16[4,3,32,256]{3,2,1,0:T(8,128)(2,1)S(1)} %collective-permute-done.yeven, bf16[4,3,32,256]{3,2,1,0:T(8,128)(2,1)S(1)} %collective-permute-done.1.yodd, ...), custom_call_target="tpu_custom_call" | custom-call | flops 100000000 | bytes 3336192 | tf_op jit(solution)/shard_map/pallas_call | solution.py:37
  11.5 1.9 %collective-permute-start.3 = (bf16[3,14,32,256]{3,2,1,0:T(8,128)(2,1)S(1)}, bf16[3,14,32,256]{3,2,1,0:T(8,128)(2,1)S(1)}, u32[]{:S(2)}, u32[]{:S(2)}) collective-permute-start(bf16[3,14,32,256]{3,2,1,0:T(8,128)(2,1)S(1)} %get-tuple-element.65), channel_id=1, source_target_pairs={{0,4},{4,0},{8,12},{12,8},{16,20},{20,16},{24,28},{28,24},{1,5},{5... | collective-permute-start | bytes 2064392 | tf_op jit(solution)/shard_map/ppermute | solution.py:32
  13.4 3.0 %collective-permute-start.4 = (bf16[2,8,32,256]{3,2,1,0:T(8,128)(2,1)S(1)}, bf16[2,8,32,256]{3,2,1,0:T(8,128)(2,1)S(1)}, u32[]{:S(2)}, u32[]{:S(2)}) collective-permute-start(bf16[2,8,32,256]{3,2,1,0:T(8,128)(2,1)S(1)} %get-tuple-element.73), channel_id=1, source_target_pairs={{4,8},{8,4},{12,16},{16,12},{20,24},{24,20},{5,9},{9,5},{13,17},{1... | collective-permute-start | bytes 786440 | tf_op jit(solution)/shard_map/ppermute | solution.py:32
  16.4 3.4 %collective-permute-start.2 = (bf16[14,32,256]{2,1,0:T(8,128)(2,1)S(1)}, bf16[14,32,256]{2,1,0:T(8,128)(2,1)S(1)}, u32[]{:S(2)}, u32[]{:S(2)}) collective-permute-start(bf16[14,32,256]{2,1,0:T(8,128)(2,1)S(1)} %get-tuple-element.64), channel_id=1, source_target_pairs={{4,8},{8,4},{12,16},{16,12},{20,24},{24,20},{5,9},{9,5},{13,17},{1... | collective-permute-start | bytes 688136 | tf_op jit(solution)/shard_map/ppermute | solution.py:32
  19.8 0.0 collective-permute-done.3.near
  19.9 4.3 %shard_map.103 = (f32[3,5,16,256]{3,2,1,0:T(8,128)S(1)}, bf16[3,2,14,32,256]{4,3,2,1,0:T(8,128)(2,1)S(1)}) custom-call(bf16[4,8,32,256]{3,2,1,0:T(8,128)(2,1)S(1)} %get-tuple-element.44.own, bf16[3,14,32,256]{3,2,1,0:T(8,128)(2,1)S(1)} %collective-permute-done.3.near, bf16[4,3,32,256]{3,2,1,0:T(8,128)(2,1)S(1)} %collective-permute-done.yeven, ...), custom_call_target="tpu_custom_call" | custom-call | flops 6000000000 | bytes 5328896 | tf_op jit(solution)/shard_map/pallas_call | solution.py:37
  24.2 0.6 %collective-permute-done.4.far = bf16[2,8,32,256]{3,2,1,0:T(8,128)(2,1)S(1)} collective-permute-done((bf16[2,8,32,256]{3,2,1,0:T(8,128)(2,1)S(1)}, bf16[2,8,32,256]{3,2,1,0:T(8,128)(2,1)S(1)}, u32[]{:S(2)}, u32[]{:S(2)}) %collective-permute-start.4) | collective-permute-done | bytes 262176 | tf_op jit(solution)/shard_map/ppermute | solution.py:32
  24.8 1.2 %shard_map.104 = (f32[3,3,16,256]{3,2,1,0:T(8,128)S(1)}, bf16[3,2,8,32,256]{4,3,2,1,0:T(8,128)(2,1)S(1)}) custom-call(bf16[2,8,32,256]{3,2,1,0:T(8,128)(2,1)S(1)} %collective-permute-done.4.far, bf16[3,2,14,32,256]{4,3,2,1,0:T(8,128)(2,1)S(1)} %get-tuple-element.72.tail, bf16[192,768]{1,0:T(8,128)(2,1)S(1)} %get-tuple-element.66.wxy, ...), custom_call_target="tpu_custom_call" | custom-call | flops 3000000000 | bytes 4538368 | tf_op jit(solution)/shard_map/pallas_call | solution.py:37
  25.9 3.2 %collective-permute-done.2.corner = bf16[14,32,256]{2,1,0:T(8,128)(2,1)S(1)} collective-permute-done((bf16[14,32,256]{2,1,0:T(8,128)(2,1)S(1)}, bf16[14,32,256]{2,1,0:T(8,128)(2,1)S(1)}, u32[]{:S(2)}, u32[]{:S(2)}) %collective-permute-start.2) | collective-permute-done | bytes 229408 | tf_op jit(solution)/shard_map/ppermute | solution.py:32
  29.1 1.6 %shard_map.105 = f32[3,4,8,256]{3,2,1,0:T(8,128)} custom-call(bf16[14,32,256]{2,1,0:T(8,128)(2,1)S(1)} %collective-permute-done.2.corner, bf16[3,2,14,32,256]{4,3,2,1,0:T(8,128)(2,1)S(1)} %get-tuple-element.72.tail, bf16[3,2,8,32,256]{4,3,2,1,0:T(8,128)(2,1)S(1)} %get-tuple-element.76.face, f32[3,5,16,256]{3,2,1,0:T(8,128)S(1)} %get-tuple-element.77.mean, ...), custom_call_target="tpu_custom_call" | custom-call | flops 2000000000 | bytes 4263936 | tf_op jit(solution)/shard_map/pallas_call | solution.py:37
Async XLA Ops:
  1.6 5.9 %collective-permute-start = (bf16[4,3,32,256]{3,2,1,0:T(8,128)(2,1)S(1)}, bf16[4,3,32,256]{3,2,1,0:T(8,128)(2,1)S(1)}, u32[]{:S(2)}, u32[]{:S(2)}) collective-permute-start(bf16[4,3,32,256]{3,2,1,0:T(8,128)(2,1)S(1)} %get-tuple-element.45), channel_id=1, source_target_pairs={{0,1},{1,0},{2,3},{3,2},{4,5},{5,4},{6,7},{7,6},{8,9},{9,8},{10,11... | collective-permute-start | bytes 589832 | tf_op jit(solution)/shard_map/ppermute | solution.py:32
  2.9 7.4 %collective-permute-start.1 = (bf16[4,3,32,256]{3,2,1,0:T(8,128)(2,1)S(1)}, bf16[4,3,32,256]{3,2,1,0:T(8,128)(2,1)S(1)}, u32[]{:S(2)}, u32[]{:S(2)}) collective-permute-start(bf16[4,3,32,256]{3,2,1,0:T(8,128)(2,1)S(1)} %get-tuple-element.46), channel_id=1, source_target_pairs={{1,2},{2,1},{5,6},{6,5},{9,10},{10,9},{13,14},{14,13},{17,18},{18,... | collective-permute-start | bytes 589832 | tf_op jit(solution)/shard_map/ppermute | solution.py:32
  11.5 8.3 %collective-permute-start.3 = (bf16[3,14,32,256]{3,2,1,0:T(8,128)(2,1)S(1)}, bf16[3,14,32,256]{3,2,1,0:T(8,128)(2,1)S(1)}, u32[]{:S(2)}, u32[]{:S(2)}) collective-permute-start(bf16[3,14,32,256]{3,2,1,0:T(8,128)(2,1)S(1)} %get-tuple-element.65), channel_id=1, source_target_pairs={{0,4},{4,0},{8,12},{12,8},{16,20},{20,16},{24,28},{28,24},{1,5},{5... | collective-permute-start | bytes 2064392 | tf_op jit(solution)/shard_map/ppermute | solution.py:32
  13.4 11.4 %collective-permute-start.4 = (bf16[2,8,32,256]{3,2,1,0:T(8,128)(2,1)S(1)}, bf16[2,8,32,256]{3,2,1,0:T(8,128)(2,1)S(1)}, u32[]{:S(2)}, u32[]{:S(2)}) collective-permute-start(bf16[2,8,32,256]{3,2,1,0:T(8,128)(2,1)S(1)} %get-tuple-element.73), channel_id=1, source_target_pairs={{4,8},{8,4},{12,16},{16,12},{20,24},{24,20},{5,9},{9,5},{13,17},{1... | collective-permute-start | bytes 786440 | tf_op jit(solution)/shard_map/ppermute | solution.py:32
  16.4 12.7 %collective-permute-start.2 = (bf16[14,32,256]{2,1,0:T(8,128)(2,1)S(1)}, bf16[14,32,256]{2,1,0:T(8,128)(2,1)S(1)}, u32[]{:S(2)}, u32[]{:S(2)}) collective-permute-start(bf16[14,32,256]{2,1,0:T(8,128)(2,1)S(1)} %get-tuple-element.64), channel_id=1, source_target_pairs={{4,8},{8,4},{12,16},{16,12},{20,24},{24,20},{5,9},{9,5},{13,17},{1... | collective-permute-start | bytes 688136 | tf_op jit(solution)/shard_map/ppermute | solution.py:32
